TPU v7x, 128 devices: a whole 4x4x4 slice. The times are simulated.
128 devices in a mesh: dp: 1, tp: 16 (over z, y), dm: 8 (over x, core).
Axes of the slice: x: 4, y: 4, z: 4, core: 2. Of those that a mesh axis runs over, the one named last changes fastest.
Arguments:
- resid_in: bfloat16 [1536, 3072], P('dp', 'dm')
- k_cache: bfloat16 [1536, 16, 16, 256], P(('dp', 'dm'), 'tp')
- v_cache: bfloat16 [1536, 16, 16, 256], P(('dp', 'dm'), 'tp')
- cache_len: int32 [1536], P('dp')
- norm_attn: bfloat16 [3072], P('dm')
- w_q: bfloat16 [3072, 4096], P('dm', 'tp')
- w_k: bfloat16 [3072, 4096], P('dm', 'tp')
- w_v: bfloat16 [3072, 4096], P('dm', 'tp')
- w_o: bfloat16 [4096, 3072], P('tp', 'dm')
- norm_mlp: bfloat16 [3072], P('dm')
- w_gate: bfloat16 [3072, 24576], P('dm', 'tp')
- w_up: bfloat16 [3072, 24576], P('dm', 'tp')
- w_down: bfloat16 [24576, 3072], P('tp', 'dm')
Outputs:
- output 1: bfloat16 [1536, 3072], P('dp', 'dm')
- output 2: bfloat16 [1536, 16, 16, 256], P(('dp', 'dm'), 'tp')
- output 3: bfloat16 [1536, 16, 16, 256], P(('dp', 'dm'), 'tp')
All inputs are finite; a program needn't handle non-finite values.
Results may differ from a plain program's by a relative error of at most 0.010591.
Values are sent between devices in bfloat16 or wider.
A program may use at most 1 GiB of HBM per device.

v0:
```python
import math

import jax
import jax.numpy as jnp
from jax import lax
from jax.experimental import pallas as pl
from jax.experimental.pallas import tpu as pltpu
from jax.sharding import PartitionSpec as P

EPSILON = 1e-6
ROPE_THETA = 10000.0
BF = jnp.bfloat16
F32 = jnp.float32
LOGICAL = pl.DeviceIdType.LOGICAL


class Comm:
    def __init__(self, wait_buf, sems):
        self.wait_buf, self.sems = wait_buf, list(sems)
        self.groups = []
        tp, dm = lax.axis_index('tp'), lax.axis_index('dm')
        self.tp, self.dm = tp, dm
        self.z, self.y = lax.div(tp, 4), lax.rem(tp, 4)
        self.x, self.c = lax.div(dm, 2), lax.rem(dm, 2)
        self.other = tp * 8 + self.x * 2 + 1 - self.c
        self.rings = {}
        for axis, me, base, step in (('x', self.x, tp * 8 + self.c, 2), ('y', self.y, self.z * 32 + dm, 8), ('z', self.z, self.y * 8 + dm, 32)):
            idx = [me] + [lax.rem(me + k, 4) for k in (1, 2, 3)]
            self.rings[axis] = idx, base + idx[1] * step, base + idx[3] * step

    def neighbours(self):
        return [self.other] + [d for r in self.rings.values() for d in r[1:]]

    def barrier(self, peers):
        sem = pltpu.get_barrier_semaphore()
        for dev in peers:
            pl.semaphore_signal(sem, inc=1, device_id=dev, device_id_type=LOGICAL)
        pl.semaphore_wait(sem, len(peers))

    def send(self, src, dst, dev):
        rows = math.prod(dst.shape) * dst.dtype.itemsize // 256
        if not self.groups or self.groups[-1][1] + rows > self.wait_buf.shape[0]:
            self.groups.append([self.sems.pop(), 0])
        self.groups[-1][1] += rows
        recv = self.sems.pop()
        pltpu.make_async_remote_copy(src_ref=src, dst_ref=dst, send_sem=self.groups[-1][0], recv_sem=recv, device_id=dev, device_id_type=LOGICAL).start()
        return recv, rows

    def wait(self, *copies):
        for sem, rows in copies:
            part = self.wait_buf.at[0:rows]
            pltpu.make_async_copy(part, part, sem).wait()

    def local(self, src, dst):
        rows = math.prod(dst.shape) * dst.dtype.itemsize // 256
        sem = self.sems.pop()
        pltpu.make_async_copy(src, dst, sem).start()
        return sem, rows

    def drain(self):
        self.wait(*self.groups)


def run(*gens):
    gens = list(gens)
    while gens:
        for g in list(gens):
            try:
                next(g)
            except StopIteration:
                gens.remove(g)


def gather4(cm, axis, blk, hf, fine=True):
    (i, r, o, l), dr, dl = cm.rings[axis]
    if fine:
        a0 = cm.send(hf(i, 0), hf(i, 0), dr)
        b1 = cm.send(hf(i, 1), hf(i, 1), dl)
        a1 = cm.send(hf(i, 1), hf(i, 1), dr)
        b0 = cm.send(hf(i, 0), hf(i, 0), dl)
        late = (a1, b0)
    else:
        a0 = cm.send(blk(i), blk(i), dr)
        b1 = cm.send(blk(i), blk(i), dl)
        late = ()
    yield
    cm.wait(a0)
    c = cm.send(hf(l, 0), hf(l, 0), dr)
    cm.wait(b1)
    d = cm.send(hf(r, 1), hf(r, 1), dl)
    yield
    cm.wait(*late)
    yield
    cm.wait(c, d)


def scatter4(cm, axis, blk, hf, rx, hrx):
    (i, r, o, l), dr, dl = cm.rings[axis]
    ro0, ro1, rl, rr = rx
    c0 = cm.send(hf(o, 0), ro0, dr)
    c1 = cm.send(hf(o, 1), ro1, dl)
    c2 = cm.send(hf(r, 1), hrx(rl, 1), dr)
    c3 = cm.send(hf(l, 0), hrx(rr, 0), dl)
    yield
    cm.wait(c0)
    hf(r, 0)[...] += ro0[...]
    c4 = cm.send(hf(r, 0), hrx(rl, 0), dr)
    cm.wait(c1)
    hf(l, 1)[...] += ro1[...]
    c5 = cm.send(hf(l, 1), hrx(rr, 1), dl)
    yield
    cm.wait(c2, c3, c4, c5)
    blk(i)[...] += rl[...] + rr[...]


def rows48(j, start=0, size=48, align=8):
    return pl.ds(pl.multiple_of(j * 48 + start, align), size)


def plane_scatter(cm, p, h, rx):
    y = (lambda j: p.at[:, rows48(j)]), (lambda j, s: p.at[2 * s:2 * s + 2, rows48(j)]), rx[:4], (lambda b, s: b.at[2 * s:2 * s + 2])
    z = (lambda j: p.at[j]), (lambda j, s: p.at[j, 96 * s:96 * s + 96]), rx[:4], (lambda b, s: b.at[96 * s:96 * s + 96])
    ys = (lambda j: p.at[cm.z, rows48(j)]), (lambda j, s: p.at[cm.z, rows48(j, 24 * s, 24)]), rx[4:], (lambda b, s: b.at[24 * s:24 * s + 24])
    zs = (lambda j: p.at[j, rows48(cm.y)]), (lambda j, s: p.at[j, rows48(cm.y, 24 * s, 24)]), rx[4:], (lambda b, s: b.at[24 * s:24 * s + 24])
    if h == 0:
        yield from scatter4(cm, 'y', *y)
        yield from scatter4(cm, 'z', *zs)
    else:
        yield from scatter4(cm, 'z', *z)
        yield from scatter4(cm, 'y', *ys)


def scatter_scratch():
    V = pltpu.VMEM
    small = [V((24, 384), F32)] * 2 + [V((48, 384), F32)] * 2
    return [V((2, 48, 384), F32)] * 2 + [V((4, 48, 384), F32)] * 2 + small + [V((96, 384), F32)] * 2 + [V((192, 384), F32)] * 2 + small


def plane_gather(cm, m, h, split, near=None, fine=(False, True)):
    cols = m.shape[-1]
    cut = lambda s: pl.ds(0, split) if s == 0 else pl.ds(split, cols - split)
    at = lambda j: rows48(j, align=16)
    if h == 0:
        first, second = 'y', 'z'
        blk, hf = (lambda j: m.at[cm.z, at(j)]), (lambda j, s: m.at[cm.z, at(j), cut(s)])
        big, bigh = (lambda j: m.at[j]), (lambda j, s: m.at[j, 96 * s:96 * s + 96])
    else:
        first, second = 'z', 'y'
        blk, hf = (lambda j: m.at[j, at(cm.y)]), (lambda j, s: m.at[j, at(cm.y), cut(s)])
        big, bigh = (lambda j: m.at[:, at(j)]), (lambda j, s: m.at[2 * s:2 * s + 2, at(j)])
    yield from gather4(cm, first, blk, hf, fine[0])
    i, r, o, l = cm.rings[second][0]
    g = gather4(cm, second, big, bigh, fine[1])
    next(g)
    yield
    next(g)
    yield
    if near:
        near(i)
    yield
    next(g)
    if near:
        near(l)
        near(r)
    yield
    for _ in g:
        pass
    if near:
        near(o)


def gain_row(g_ref, d, k):
    g = g_ref[d]
    return jnp.concatenate([g[3 * k + j:3 * k + j + 1] for j in range(3)], axis=1)


def qkv_kernel(x_ref, wq_ref, wk_ref, wv_ref, ga_ref, gm_ref, q_ref, k_ref, v_ref, g_ref, w_buf, xg, n_buf, gain_buf, wait_buf, *sems):
    cm = Comm(wait_buf, sems)
    x, c, dm = cm.x, cm.c, cm.dm
    peers = [cm.tp * 8 + lax.rem(dm + k, 8) for k in range(1, 8)]
    cm.barrier(peers + [d for a in 'yz' for d in cm.rings[a][1:]])

    sl = jnp.where(c == 0, cm.y, cm.z)
    xs = []
    for k, dev in enumerate(peers):
        start = pl.multiple_of(lax.rem(dm + k + 1, 8) * 192 + sl * 48, 16)
        xs.append(cm.send(x_ref.at[pl.ds(start, 48), :], xg.at[c, sl, x], dev))
    gain_buf[0:3] = ga_ref[...].astype(F32)
    gain_buf[3:6] = gm_ref[...].astype(F32)
    gain_buf[6:8] = jnp.zeros((2, 128), F32)
    (i, r, o, l), dr, dl = cm.rings['x']
    dev_o = cm.other
    rows = lambda j: w_buf.at[j * 2 + c]
    ws = (wq_ref, wk_ref, wv_ref)
    lo, hi, full = pl.ds(0, 192), pl.ds(192, 192), pl.ds(0, 384)
    pieces = ((0, full), (1, lo), (1, hi), (2, full))
    a = [cm.send(ws[n].at[p], rows(i).at[n, p], dr) for n, p in pieces]
    b = [cm.send(ws[n].at[p], rows(i).at[n, p], dl) for n, p in pieces[::-1]]
    e = [cm.send(w, rows(i).at[n], dev_o) for n, w in enumerate(ws)]
    gs = [cm.send(gain_buf, g_ref.at[dm], dev) for dev in peers]
    mine = [cm.local(w, w_buf.at[dm, n]) for n, w in enumerate(ws)]
    own = pl.multiple_of(dm * 192 + sl * 48, 16)
    xs.append(cm.local(x_ref.at[pl.ds(own, 48), :], xg.at[c, sl, x]))
    g_ref[dm] = gain_buf[...]
    cm.wait(*xs)

    def on(cps, src, ps, dev):
        f = []
        for cp, (n, p) in zip(cps, ps):
            cm.wait(cp)
            f.append(cm.send(rows(src).at[n, p], rows(src).at[n, p], dev))
        return f

    gy = gather4(cm, 'y', lambda j: xg.at[0, j], lambda j, s: xg.at[0, j, 2 * s:2 * s + 2])
    gz = gather4(cm, 'z', lambda j: xg.at[1, j], lambda j, s: xg.at[1, j, 2 * s:2 * s + 2])
    for g in (gy, gz, gy, gz):
        next(g)
    f0 = on(a[:2], l, pieces[:2], dr)
    f1 = on(b[:2], r, pieces[::-1][:2], dl)
    run(gy, gz)
    cm.wait(*gs)
    total = jnp.zeros((192, 1), F32)
    for d in range(8):
        v = xg[d % 2, :, d // 2].reshape(192, 384).astype(F32)
        total += jnp.sum(v * v, axis=1, keepdims=True)
    inv = lax.rsqrt(total / 3072 + EPSILON)
    for d in range(8):
        v = xg[d % 2, :, d // 2].reshape(192, 384).astype(F32)
        n_buf[d] = (v * inv * (1.0 + gain_row(g_ref, d, 0))).astype(BF)
    outs = (q_ref, k_ref, v_ref)

    def add(j, first=False):
        for n, out in enumerate(outs):
            part = jnp.dot(n_buf[j * 2], w_buf[j * 2, n], preferred_element_type=F32) + jnp.dot(n_buf[j * 2 + 1], w_buf[j * 2 + 1, n], preferred_element_type=F32)
            out[...] = part if first else out[...] + part

    cm.wait(*e, *mine)
    add(i, True)
    cm.wait(*a[2:])
    e1 = cm.send(rows(l), rows(l), dev_o)
    cm.wait(*b[2:])
    e2 = cm.send(rows(r), rows(r), dev_o)
    cm.wait(e1)
    add(l)
    cm.wait(e2)
    add(r)
    cm.wait(*f0, *f1)
    cm.wait(cm.send(rows(o), rows(o), dev_o))
    add(o)
    cm.drain()


def post_kernel(o_ref, x_ref, wo_ref, wg_ref, wu_ref, wd_ref, g_ref, u_out, v_out, o_buf, wo, x_o, wd, pa, pb, pc, pd, hs, ma, mb, acc_a, acc_b, w_gu, ta, tb, tc, td, a_buf, u_buf, wait_buf, *rest):
    rx, rx2, sems = rest[:16], rest[16:32], rest[32:]
    cm = Comm(wait_buf, sems)
    x, c, y, z = cm.x, cm.c, cm.y, cm.z
    (i, r, o, l), dr, dl = cm.rings['x']
    dev_o = cm.other
    cm.barrier(cm.neighbours())

    o_buf[x] = o_ref[...]
    go = gather4(cm, 'x', lambda j: o_buf.at[j], lambda j, s: o_buf.at[j, 96 * s:96 * s + 96])
    next(go)
    row = lambda core: pl.multiple_of(192 * (2 * z + core) + 48 * y, 16)
    c_wo = cm.send(wo_ref, wo.at[c], dev_o)
    c_x = cm.send(x_ref.at[pl.ds(row(1 - c), 48), :], x_o, dev_o)
    c_wd = cm.send(wd_ref, wd.at[c], dev_o)
    wo[c] = wo_ref[...]
    own_wd = cm.local(wd_ref, wd.at[c])
    kblk = lambda j: pl.ds(pl.multiple_of((j * 2 + c) * 384, 16), 384)
    hcol = lambda j: pl.ds(pl.multiple_of(j * 384, 128), 384)

    def deal(w_ref, col, t0, t1):
        to = pl.ds(col, 384)
        half = lambda j, s: pl.ds(pl.multiple_of((j * 2 + c) * 384 + 192 * s, 16), 192)
        c_own = cm.send(w_ref.at[:, hcol(i)], w_gu.at[kblk(i), to], dev_o)
        c0 = cm.send(w_ref.at[0:192, hcol(o)], t0, dr)
        c1 = cm.send(w_ref.at[192:384, hcol(o)], t1, dl)
        c_r = cm.send(w_ref.at[:, hcol(r)], w_gu.at[kblk(i), to], dr)
        c_l = cm.send(w_ref.at[:, hcol(l)], w_gu.at[kblk(i), to], dl)
        own = cm.local(w_ref.at[:, hcol(i)], w_gu.at[kblk(i), to])
        yield
        yield
        cm.wait(c0)
        f0 = cm.send(t0, w_gu.at[half(l, 0), to], dr)
        cm.wait(c1)
        f1 = cm.send(t1, w_gu.at[half(r, 1), to], dl)
        yield
        yield
        cm.wait(c_r)
        e1 = cm.send(w_gu.at[kblk(l), to], w_gu.at[kblk(l), to], dev_o)
        cm.wait(c_l)
        e2 = cm.send(w_gu.at[kblk(r), to], w_gu.at[kblk(r), to], dev_o)
        cm.wait(f0, f1)
        e3 = cm.send(w_gu.at[kblk(o), to], w_gu.at[kblk(o), to], dev_o)
        yield
        cm.wait(c_own, own, e1, e2, e3)

    for _ in go:
        pass
    deal_g = deal(wg_ref, 0, ta, tb)
    next(deal_g)
    cm.wait(c_wo)

    def o_proj(j, carry):
        v = o_buf[j]
        pa[j] = jnp.dot(v, wo[0], preferred_element_type=F32)
        pb[j] = jnp.dot(v, wo[1], preferred_element_type=F32)
        return carry

    lax.fori_loop(0, 4, o_proj, 0)
    run(plane_scatter(cm, pa, 0, rx[:8]), plane_scatter(cm, pb, 1, rx[8:]), deal_g)

    cm.wait(c_x)
    mine, theirs = x_ref[pl.ds(row(c), 48), :].astype(F32), x_o[...].astype(F32)
    first = c == 0
    hs[x, 0] = (jnp.where(first, mine, theirs) + pa[z, rows48(y)]).astype(BF)
    hs[x, 1] = (jnp.where(first, theirs, mine) + pb[z, rows48(y)]).astype(BF)
    run(gather4(cm, 'x', lambda j: hs.at[j], lambda j, s: hs.at[j, s]))
    deal_u = deal(wu_ref, 384, tc, td)
    next(deal_u)
    total = jnp.zeros((48, 1), F32)
    for d in range(8):
        v = hs[d // 2, d % 2].astype(F32)
        total += jnp.sum(v * v, axis=1, keepdims=True)
    inv = lax.rsqrt(total / 3072 + EPSILON)
    for d in range(8):
        v = hs[d // 2, d % 2].astype(F32)
        (ma, mb)[d // 4][z, rows48(y, align=16), 384 * (d % 4):384 * (d % 4) + 384] = (v * inv * (1.0 + gain_row(g_ref, d, 1))).astype(BF)

    def part_a(j):
        acc_a[j] = jnp.dot(ma[j], w_gu[0:1536], preferred_element_type=F32)

    def part_b(j):
        acc_b[:, rows48(j)] = jnp.dot(mb[:, rows48(j, align=16)].reshape(192, 1536), w_gu[1536:3072], preferred_element_type=F32).reshape(4, 48, 768)

    run(plane_gather(cm, ma, 0, 768, part_a), plane_gather(cm, mb, 1, 768, part_b), deal_u)

    def hidden(j):
        s = acc_a[j] + acc_b[j]
        gate, up = s[:, 0:384], s[:, 384:768]
        gelu = 0.5 * gate * (1.0 + jnp.tanh(0.7978845608 * (gate + 0.044715 * (gate * gate * gate))))
        a_buf[j, :, hcol(x)] = (gelu * up).astype(BF)

    right, left = {}, {}
    for j in (0, 2, 1, 3):
        hidden(j)
        own = a_buf.at[j, :, hcol(x)]
        right[j] = cm.send(own, own, dr)
        left[j] = cm.send(own, own, dl)
    fwd = []
    for j in (0, 1):
        cm.wait(right[j])
        src = a_buf.at[j, :, hcol(l)]
        fwd.append(cm.send(src, src, dr))
        cm.wait(left[j + 2])
        src = a_buf.at[j + 2, :, hcol(r)]
        fwd.append(cm.send(src, src, dl))
    cm.wait(right[2], right[3], left[0], left[1], c_wd, own_wd)
    for j, k in ((0, 0), (2, 1), (1, 2), (3, 3)):
        cm.wait(fwd[k])
        v = a_buf[j]
        pc[j] = jnp.dot(v, wd[0], preferred_element_type=F32)
        pd[j] = jnp.dot(v, wd[1], preferred_element_type=F32)
    run(plane_scatter(cm, pc, 0, rx2[:8]), plane_scatter(cm, pd, 1, rx2[8:]))
    u_buf[0, z, rows48(y, align=16)] = (hs[x, 0].astype(F32) + pc[z, rows48(y)]).astype(BF)
    u_buf[1, z, rows48(y, align=16)] = (hs[x, 1].astype(F32) + pd[z, rows48(y)]).astype(BF)
    run(plane_gather(cm, u_buf.at[0], 0, 256, None, (False, False)), plane_gather(cm, u_buf.at[1], 1, 256, None, (False, False)))
    c_v = cm.send(u_buf.at[1 - c], v_out, dev_o)
    u_out[...] = u_buf[c]
    cm.wait(c_v)
    cm.drain()


def rope_rotate(vectors, positions):
    half_dim = vectors.shape[-1] // 2
    inv_freq = ROPE_THETA ** (-2.0 * jnp.arange(half_dim, dtype=jnp.float32) / vectors.shape[-1])
    angles = positions.astype(jnp.float32)[:, None] * inv_freq[None, :]
    cos_part = jnp.cos(angles)[:, None, :]
    sin_part = jnp.sin(angles)[:, None, :]
    first_half = vectors[..., :half_dim]
    second_half = vectors[..., half_dim:]
    return jnp.concatenate([first_half * cos_part - second_half * sin_part, second_half * cos_part + first_half * sin_part], axis=-1)


def attend(q_rot, k_cache, v_cache, k_new, v_new, lengths):
    slot_ids = jnp.arange(k_cache.shape[2])
    slot_hit = slot_ids[None, :] == lengths[:, None]
    valid_mask = slot_ids[None, :] <= lengths[:, None]
    k_upd = jnp.where(slot_hit[:, None, :, None], k_new[:, :, None, :], k_cache)
    v_upd = jnp.where(slot_hit[:, None, :, None], v_new[:, :, None, :], v_cache)
    scores = jnp.einsum('bhe,bhte->bht', q_rot, k_upd, preferred_element_type=jnp.float32)
    scores = jnp.where(valid_mask[:, None, :], scores, -1e30)
    attn_probs = jax.nn.softmax(scores, axis=-1).astype(jnp.bfloat16)
    attn_out = jnp.einsum('bht,bhte->bhe', attn_probs, v_upd, preferred_element_type=jnp.float32)
    return attn_out.astype(jnp.bfloat16), k_upd, v_upd


VM = pl.BlockSpec(memory_space=pltpu.VMEM)
VMEM_LIMIT = 60 * 1024 * 1024


ANY = pl.BlockSpec(memory_space=pl.ANY)


def call(body, outs, scratch, sems, cid, flops, where, *args):
    single = len(outs) == 1
    return pl.pallas_call(
        body,
        out_shape=outs[0] if single else outs,
        in_specs=[ANY if w == 'h' else VM for w in where],
        out_specs=VM if single else [VM] * len(outs),
        scratch_shapes=scratch + [pltpu.SemaphoreType.DMA] * sems,
        compiler_params=pltpu.CompilerParams(collective_id=cid, has_side_effects=True, vmem_limit_bytes=VMEM_LIMIT),
        cost_estimate=pl.CostEstimate(flops=flops, bytes_accessed=8_000_000, transcendentals=0),
    )(*args)


def call2(body, outs, scratch, sems, cid, flops, where, *args):
    single = len(outs) == 1
    return pl.pallas_call(
        body,
        out_shape=outs[0] if single else outs,
        in_specs=[ANY if w == 'h' else VM for w in where],
        out_specs=VM if single else [VM] * len(outs),
        scratch_shapes=scratch + [pltpu.SemaphoreType.DMA] * sems,
        compiler_params=pltpu.CompilerParams(collective_id=cid, has_side_effects=True, vmem_limit_bytes=VMEM_LIMIT),
        cost_estimate=pl.CostEstimate(flops=flops, bytes_accessed=8_000_000, transcendentals=0),
    )(*args)


def join_kernel(u_ref, v_ref, out_ref):
    c = lax.rem(lax.axis_index('dm'), 2)
    for j in range(4):
        out_ref[pl.ds(pl.multiple_of(192 * (2 * j + c), 16), 192), :] = u_ref[j]
        out_ref[pl.ds(pl.multiple_of(192 * (2 * j + 1 - c), 16), 192), :] = v_ref[j]


def solution(mesh):
    cache_spec = P(('dp', 'dm'), 'tp', None, None)
    resid_spec = P('dp', 'dm')
    col_spec = P('dm', 'tp')
    row_spec = P('tp', 'dm')
    in_specs = (resid_spec, cache_spec, cache_spec, P('dp'), P('dm'), col_spec, col_spec, col_spec, row_spec, P('dm'), col_spec, col_spec, row_spec)
    out_specs = (resid_spec, cache_spec, cache_spec)
    sds = jax.ShapeDtypeStruct
    V = pltpu.VMEM

    def local_step(resid_in, k_cache, v_cache, cache_len, norm_attn, w_q, w_k, w_v, w_o, norm_mlp, w_gate, w_up, w_down):
        lengths = lax.dynamic_slice_in_dim(cache_len, lax.axis_index('dm') * 192, 192)
        q_sum, k_sum, v_sum, gain_all = call(
            qkv_kernel,
            (sds((192, 256), F32),) * 3 + (sds((8, 8, 128), F32),),
            [V((8, 3, 384, 256), BF), V((2, 4, 4, 48, 384), BF), V((8, 192, 384), BF), V((8, 128), F32), V((8192, 128), BF)],
            60, 0, 2 * 10**9, 'hhhhvv',
            resid_in, w_q, w_k, w_v, norm_attn.reshape(3, 128), norm_mlp.reshape(3, 128))
        heads = lambda a: a.reshape(192, 1, 256)
        q_rot = (rope_rotate(heads(q_sum), lengths) * 256 ** -0.5).astype(BF)
        k_new = rope_rotate(heads(k_sum), lengths).astype(BF)
        v_new = heads(v_sum).astype(BF)
        attn_out, k_upd, v_upd = attend(q_rot, k_cache, v_cache, k_new, v_new, lengths)
        mine, theirs = call2(
            post_kernel,
            (sds((4, 192, 384), BF), sds((4, 192, 384), BF)),
            [V((4, 192, 256), BF), V((2, 256, 384), BF), V((48, 384), BF), V((2, 1536, 384), BF)]
            + [V((4, 192, 384), F32)] * 4 + [V((4, 2, 48, 384), BF)] + [V((4, 192, 1536), BF)] * 2 + [V((4, 192, 768), F32)] * 2
            + [V((3072, 768), BF)] + [V((192, 384), BF)] * 4 + [V((4, 192, 1536), BF), V((2, 4, 192, 384), BF), V((16384, 128), BF)]
            + scatter_scratch() + scatter_scratch(),
            170, 1, 7 * 10**9, 'vvvhhhv',
            attn_out.reshape(192, 256), resid_in, w_o, w_gate, w_up, w_down, gain_all)
        resid_out = pl.pallas_call(join_kernel, out_shape=sds((1536, 384), BF), in_specs=[VM, VM], out_specs=VM)(mine, theirs)
        return resid_out, k_upd, v_upd

    return jax.shard_map(local_step, mesh=mesh, in_specs=in_specs, out_specs=out_specs, check_vma=False)
```

profile of v0, /device:TPU:1, one launch (start us, length us, event | category | flops | bytes accessed | tf_op | source)
XLA Modules:
  0.0 169.5 jit_solution(10165638775312376342)
XLA Ops:
  0.6 0.8 fusion.30
  1.4 0.1 iota_compare_fusion
  1.5 0.0 copy-start.1
  1.5 0.0 copy-start.2
  1.6 35.3 %shard_map.148 = (f32[192,256]{1,0:T(8,128)}, f32[192,256]{1,0:T(8,128)}, f32[192,256]{1,0:T(8,128)}, f32[8,8,128]{2,1,0:T(8,128)}) custom-call(bf16[1536,384]{1,0:T(8,128)(2,1)} %x_ref.3, bf16[384,256]{1,0:T(8,128)(2,1)} %wq_ref.1, bf16[384,256]{1,0:T(8,128)(2,1)} %wk_ref.1, bf16[384,256]{1,0:T(8,128)(2,1)} %wv_ref.1, bf16[3,128]{1,0:T(4,128)(2,1)} %bitcast.33, ...), custom_call_target="tpu_custom_call" | custom-call | flops 2000000000 | bytes 8000000 | tf_op jit(solution)/shard_map/pallas_call | solution.py:408
  36.8 1.5 fusion.15
  38.4 0.9 convert_element_type.32
  39.3 0.0 copy-done.1
  39.3 0.0 copy-done.2
  39.3 0.9 broadcast_select_fusion.1
  40.2 0.0 copy-start
  40.2 0.0 copy-start.3
  40.2 0.5 fusion.2
  40.7 0.2 fusion.25
  40.9 0.2 fusion.26
  41.2 0.2 fusion.27
  41.3 0.4 fusion
  41.7 0.0 copy-done
  41.7 0.2 copy-done.3
  41.9 0.7 copy.25
  42.5 124.6 %shard_map.149 = (bf16[4,192,384]{2,1,0:T(8,128)(2,1)}, bf16[4,192,384]{2,1,0:T(8,128)(2,1)}) custom-call(bf16[192,256]{1,0:T(8,128)(2,1)} %bitcast.32, bf16[1536,384]{1,0:T(8,128)(2,1)} %x_ref.3, bf16[256,384]{1,0:T(8,128)(2,1)} %wo_ref.1, bf16[384,1536]{1,0:T(8,128)(2,1)} %wg_ref.1, bf16[384,1536]{1,0:T(8,128)(2,1)} %wu_ref.1, bf16[1536,384]{1,0:T(8,128)(2,1)} %wd_ref.1, ...), custom_call_target="tpu_custom_call" | custom-call | flops 7000000000 | bytes 8000000 | tf_op jit(solution)/shard_map/pallas_call | solution.py:421
  167.1 2.4 %shard_map.150 = bf16[1536,384]{1,0:T(8,128)(2,1)} custom-call(bf16[4,192,384]{2,1,0:T(8,128)(2,1)} %get-tuple-element.13.u_ref, bf16[4,192,384]{2,1,0:T(8,128)(2,1)} %get-tuple-element.14.v_ref), custom_call_target="tpu_custom_call" | custom-call | tf_op jit(solution)/shard_map/pallas_call | solution.py:471
  (3 shorter events, 0.0 us)
Async XLA Ops:
  1.5 37.8 %copy-start.1 = (bf16[192,1,16,256]{3,2,1,0:T(8,128)(2,1)S(1)}, bf16[192,1,16,256]{3,2,1,0:T(8,128)(2,1)}, u32[]{:S(2)}) copy-start(bf16[192,1,16,256]{3,2,1,0:T(8,128)(2,1)} %param.14) | copy-start | bytes 4718596
  1.5 37.8 %copy-start.2 = (bf16[192,1,16,256]{3,2,1,0:T(8,128)(2,1)S(1)}, bf16[192,1,16,256]{3,2,1,0:T(8,128)(2,1)}, u32[]{:S(2)}) copy-start(bf16[192,1,16,256]{3,2,1,0:T(8,128)(2,1)} %param.15) | copy-start | bytes 4718596
  40.2 1.5 copy-start
  40.2 1.7 copy-start.3
where the time goes:
time: 170 us; the launch traced here: 169 us
  Pallas kernels  162 us (95%)
  other arithmetic  4.81 us (3%)
    pallas_call x1, Pallas kernels, call2(): pl.pallas_call(body, out_shape=outs[0] if single else outs, in_specs=[ANY...  125 us
    pallas_call x1, Pallas kernels, call(): pl.pallas_call(body, out_shape=outs[0] if single else outs, in_specs=[ANY...  35.3 us

commit v1 on v0

--- a/solution.py
+++ b/solution.py
@@ -23,13 +23,14 @@
         self.z, self.y = lax.div(tp, 4), lax.rem(tp, 4)
         self.x, self.c = lax.div(dm, 2), lax.rem(dm, 2)
         self.other = tp * 8 + self.x * 2 + 1 - self.c
-        self.rings = {}
+        self.rings, self.opposite = {}, {}
         for axis, me, base, step in (('x', self.x, tp * 8 + self.c, 2), ('y', self.y, self.z * 32 + dm, 8), ('z', self.z, self.y * 8 + dm, 32)):
             idx = [me] + [lax.rem(me + k, 4) for k in (1, 2, 3)]
             self.rings[axis] = idx, base + idx[1] * step, base + idx[3] * step
+            self.opposite[axis] = base + idx[2] * step
 
     def neighbours(self):
-        return [self.other] + [d for r in self.rings.values() for d in r[1:]]
+        return [self.other] + [d for r in self.rings.values() for d in r[1:]] + list(self.opposite.values())
 
     def barrier(self, peers):
         sem = pltpu.get_barrier_semaphore()
@@ -94,6 +95,25 @@
     cm.wait(c, d)
 
 
+def direct4(cm, axis, src, dst):
+    (i, r, o, l), dr, dl = cm.rings[axis]
+    return [cm.send(src(o), dst(1), cm.opposite[axis]), cm.send(src(r), dst(0), dr), cm.send(src(l), dst(2), dl)]
+
+
+def direct_gather(cm, axis, blk):
+    own = blk(cm.rings[axis][0][0])
+    cps = direct4(cm, axis, lambda j: own, lambda k: own)
+    yield
+    cm.wait(*cps)
+
+
+def direct_scatter(cm, axis, blk, rx):
+    cps = direct4(cm, axis, blk, lambda k: rx[k])
+    yield
+    cm.wait(*cps)
+    blk(cm.rings[axis][0][0])[...] += (rx[0][...] + rx[2][...]) + rx[1][...]
+
+
 def scatter4(cm, axis, blk, hf, rx, hrx):
     (i, r, o, l), dr, dl = cm.rings[axis]
     ro0, ro1, rl, rr = rx
@@ -120,53 +140,48 @@
 def plane_scatter(cm, p, h, rx):
     y = (lambda j: p.at[:, rows48(j)]), (lambda j, s: p.at[2 * s:2 * s + 2, rows48(j)]), rx[:4], (lambda b, s: b.at[2 * s:2 * s + 2])
     z = (lambda j: p.at[j]), (lambda j, s: p.at[j, 96 * s:96 * s + 96]), rx[:4], (lambda b, s: b.at[96 * s:96 * s + 96])
-    ys = (lambda j: p.at[cm.z, rows48(j)]), (lambda j, s: p.at[cm.z, rows48(j, 24 * s, 24)]), rx[4:], (lambda b, s: b.at[24 * s:24 * s + 24])
-    zs = (lambda j: p.at[j, rows48(cm.y)]), (lambda j, s: p.at[j, rows48(cm.y, 24 * s, 24)]), rx[4:], (lambda b, s: b.at[24 * s:24 * s + 24])
     if h == 0:
         yield from scatter4(cm, 'y', *y)
-        yield from scatter4(cm, 'z', *zs)
+        yield from direct_scatter(cm, 'z', lambda j: p.at[j, rows48(cm.y)], rx[4:])
     else:
         yield from scatter4(cm, 'z', *z)
-        yield from scatter4(cm, 'y', *ys)
+        yield from direct_scatter(cm, 'y', lambda j: p.at[cm.z, rows48(j)], rx[4:])
 
 
 def scatter_scratch():
     V = pltpu.VMEM
-    small = [V((24, 384), F32)] * 2 + [V((48, 384), F32)] * 2
+    small = [V((48, 384), F32)] * 3
     return [V((2, 48, 384), F32)] * 2 + [V((4, 48, 384), F32)] * 2 + small + [V((96, 384), F32)] * 2 + [V((192, 384), F32)] * 2 + small
 
 
-def plane_gather(cm, m, h, split, near=None, fine=(False, True)):
-    cols = m.shape[-1]
-    cut = lambda s: pl.ds(0, split) if s == 0 else pl.ds(split, cols - split)
+def plane_gather(cm, m, h, near=None):
     at = lambda j: rows48(j, align=16)
     if h == 0:
-        first, second = 'y', 'z'
-        blk, hf = (lambda j: m.at[cm.z, at(j)]), (lambda j, s: m.at[cm.z, at(j), cut(s)])
+        second = 'z'
+        yield from direct_gather(cm, 'y', lambda j: m.at[cm.z, at(j)])
         big, bigh = (lambda j: m.at[j]), (lambda j, s: m.at[j, 96 * s:96 * s + 96])
     else:
-        first, second = 'z', 'y'
-        blk, hf = (lambda j: m.at[j, at(cm.y)]), (lambda j, s: m.at[j, at(cm.y), cut(s)])
+        second = 'y'
+        yield from direct_gather(cm, 'z', lambda j: m.at[j, at(cm.y)])
         big, bigh = (lambda j: m.at[:, at(j)]), (lambda j, s: m.at[2 * s:2 * s + 2, at(j)])
-    yield from gather4(cm, first, blk, hf, fine[0])
+    if near is None:
+        yield from direct_gather(cm, second, big)
+        return
     i, r, o, l = cm.rings[second][0]
-    g = gather4(cm, second, big, bigh, fine[1])
+    g = gather4(cm, second, big, bigh)
     next(g)
     yield
     next(g)
     yield
-    if near:
-        near(i)
+    near(i)
     yield
     next(g)
-    if near:
-        near(l)
-        near(r)
+    near(l)
+    near(r)
     yield
     for _ in g:
         pass
-    if near:
-        near(o)
+    near(o)
 
 
 def gain_row(g_ref, d, k):
@@ -178,13 +193,13 @@
     cm = Comm(wait_buf, sems)
     x, c, dm = cm.x, cm.c, cm.dm
     peers = [cm.tp * 8 + lax.rem(dm + k, 8) for k in range(1, 8)]
-    cm.barrier(peers + [d for a in 'yz' for d in cm.rings[a][1:]])
-
-    sl = jnp.where(c == 0, cm.y, cm.z)
-    xs = []
-    for k, dev in enumerate(peers):
-        start = pl.multiple_of(lax.rem(dm + k + 1, 8) * 192 + sl * 48, 16)
-        xs.append(cm.send(x_ref.at[pl.ds(start, 48), :], xg.at[c, sl, x], dev))
+    cm.barrier(peers + [d for a in 'yz' for d in cm.rings[a][1:] + (cm.opposite[a],)])
+
+    first = jnp.where(c == 0, cm.y, cm.z)
+    second = jnp.where(c == 0, cm.z, cm.y)
+    start = first * 48 + jnp.minimum(second, 2) * 16
+    piece = lambda d: x_ref.at[pl.ds(pl.multiple_of(d * 192 + start, 16), 16), :]
+    xs = [cm.send(piece(lax.rem(dm + k + 1, 8)), xg.at[c, first, second, x], dev) for k, dev in enumerate(peers)]
     gain_buf[0:3] = ga_ref[...].astype(F32)
     gain_buf[3:6] = gm_ref[...].astype(F32)
     gain_buf[6:8] = jnp.zeros((2, 128), F32)
@@ -199,8 +214,7 @@
     e = [cm.send(w, rows(i).at[n], dev_o) for n, w in enumerate(ws)]
     gs = [cm.send(gain_buf, g_ref.at[dm], dev) for dev in peers]
     mine = [cm.local(w, w_buf.at[dm, n]) for n, w in enumerate(ws)]
-    own = pl.multiple_of(dm * 192 + sl * 48, 16)
-    xs.append(cm.local(x_ref.at[pl.ds(own, 48), :], xg.at[c, sl, x]))
+    xs.append(cm.local(piece(dm), xg.at[c, first, second, x]))
     g_ref[dm] = gain_buf[...]
     cm.wait(*xs)
 
@@ -211,8 +225,12 @@
             f.append(cm.send(rows(src).at[n, p], rows(src).at[n, p], dev))
         return f
 
-    gy = gather4(cm, 'y', lambda j: xg.at[0, j], lambda j, s: xg.at[0, j, 2 * s:2 * s + 2])
-    gz = gather4(cm, 'z', lambda j: xg.at[1, j], lambda j, s: xg.at[1, j, 2 * s:2 * s + 2])
+    def rows_gather(k, small, big, where):
+        yield from direct_gather(cm, small, where)
+        yield from gather4(cm, big, lambda j: xg.at[k, j], lambda j, s: xg.at[k, j, :, 2 * s:2 * s + 2])
+
+    gy = rows_gather(0, 'z', 'y', lambda j: xg.at[0, cm.y, j])
+    gz = rows_gather(1, 'y', 'z', lambda j: xg.at[1, cm.z, j])
     for g in (gy, gz, gy, gz):
         next(g)
     f0 = on(a[:2], l, pieces[:2], dr)
@@ -221,11 +239,11 @@
     cm.wait(*gs)
     total = jnp.zeros((192, 1), F32)
     for d in range(8):
-        v = xg[d % 2, :, d // 2].reshape(192, 384).astype(F32)
+        v = xg[d % 2, :, 0:3, d // 2].reshape(192, 384).astype(F32)
         total += jnp.sum(v * v, axis=1, keepdims=True)
     inv = lax.rsqrt(total / 3072 + EPSILON)
     for d in range(8):
-        v = xg[d % 2, :, d // 2].reshape(192, 384).astype(F32)
+        v = xg[d % 2, :, 0:3, d // 2].reshape(192, 384).astype(F32)
         n_buf[d] = (v * inv * (1.0 + gain_row(g_ref, d, 0))).astype(BF)
     outs = (q_ref, k_ref, v_ref)
 
@@ -250,8 +268,8 @@
     cm.drain()
 
 
-def post_kernel(o_ref, x_ref, wo_ref, wg_ref, wu_ref, wd_ref, g_ref, u_out, v_out, o_buf, wo, x_o, wd, pa, pb, pc, pd, hs, ma, mb, acc_a, acc_b, w_gu, ta, tb, tc, td, a_buf, u_buf, wait_buf, *rest):
-    rx, rx2, sems = rest[:16], rest[16:32], rest[32:]
+def post_kernel(o_ref, x_ref, wo_ref, wg_ref, wu_ref, wd_ref, g_ref, u_out, v_out, o_buf, wo, x_o, wd, pa, pb, pc, pd, hs, ma, mb, acc_a, acc_b, w_gu, a_buf, u_buf, wait_buf, *rest):
+    rx, rx2, sems = rest[:14], rest[14:28], rest[28:]
     cm = Comm(wait_buf, sems)
     x, c, y, z = cm.x, cm.c, cm.y, cm.z
     (i, r, o, l), dr, dl = cm.rings['x']
@@ -259,7 +277,7 @@
     cm.barrier(cm.neighbours())
 
     o_buf[x] = o_ref[...]
-    go = gather4(cm, 'x', lambda j: o_buf.at[j], lambda j, s: o_buf.at[j, 96 * s:96 * s + 96])
+    go = direct_gather(cm, 'x', lambda j: o_buf.at[j])
     next(go)
     row = lambda core: pl.multiple_of(192 * (2 * z + core) + 48 * y, 16)
     c_wo = cm.send(wo_ref, wo.at[c], dev_o)
@@ -270,35 +288,22 @@
     kblk = lambda j: pl.ds(pl.multiple_of((j * 2 + c) * 384, 16), 384)
     hcol = lambda j: pl.ds(pl.multiple_of(j * 384, 128), 384)
 
-    def deal(w_ref, col, t0, t1):
+    def deal(w_ref, col):
         to = pl.ds(col, 384)
-        half = lambda j, s: pl.ds(pl.multiple_of((j * 2 + c) * 384 + 192 * s, 16), 192)
-        c_own = cm.send(w_ref.at[:, hcol(i)], w_gu.at[kblk(i), to], dev_o)
-        c0 = cm.send(w_ref.at[0:192, hcol(o)], t0, dr)
-        c1 = cm.send(w_ref.at[192:384, hcol(o)], t1, dl)
-        c_r = cm.send(w_ref.at[:, hcol(r)], w_gu.at[kblk(i), to], dr)
-        c_l = cm.send(w_ref.at[:, hcol(l)], w_gu.at[kblk(i), to], dl)
-        own = cm.local(w_ref.at[:, hcol(i)], w_gu.at[kblk(i), to])
+        own = w_gu.at[kblk(i), to]
+        cps = direct4(cm, 'x', lambda j: w_ref.at[:, hcol(j)], lambda k: own)
+        here = [cm.local(w_ref.at[:, hcol(i)], own), cm.send(w_ref.at[:, hcol(i)], own, dev_o)]
+        for _ in range(3):
+            yield
+        for cp, j in zip(cps[1:] + cps[:1], (l, r, o)):
+            cm.wait(cp)
+            here.append(cm.send(w_gu.at[kblk(j), to], w_gu.at[kblk(j), to], dev_o))
         yield
-        yield
-        cm.wait(c0)
-        f0 = cm.send(t0, w_gu.at[half(l, 0), to], dr)
-        cm.wait(c1)
-        f1 = cm.send(t1, w_gu.at[half(r, 1), to], dl)
-        yield
-        yield
-        cm.wait(c_r)
-        e1 = cm.send(w_gu.at[kblk(l), to], w_gu.at[kblk(l), to], dev_o)
-        cm.wait(c_l)
-        e2 = cm.send(w_gu.at[kblk(r), to], w_gu.at[kblk(r), to], dev_o)
-        cm.wait(f0, f1)
-        e3 = cm.send(w_gu.at[kblk(o), to], w_gu.at[kblk(o), to], dev_o)
-        yield
-        cm.wait(c_own, own, e1, e2, e3)
+        cm.wait(*here)
 
     for _ in go:
         pass
-    deal_g = deal(wg_ref, 0, ta, tb)
+    deal_g = deal(wg_ref, 0)
     next(deal_g)
     cm.wait(c_wo)
 
@@ -309,15 +314,15 @@
         return carry
 
     lax.fori_loop(0, 4, o_proj, 0)
-    run(plane_scatter(cm, pa, 0, rx[:8]), plane_scatter(cm, pb, 1, rx[8:]), deal_g)
+    run(plane_scatter(cm, pa, 0, rx[:7]), plane_scatter(cm, pb, 1, rx[7:]), deal_g)
 
     cm.wait(c_x)
     mine, theirs = x_ref[pl.ds(row(c), 48), :].astype(F32), x_o[...].astype(F32)
     first = c == 0
     hs[x, 0] = (jnp.where(first, mine, theirs) + pa[z, rows48(y)]).astype(BF)
     hs[x, 1] = (jnp.where(first, theirs, mine) + pb[z, rows48(y)]).astype(BF)
-    run(gather4(cm, 'x', lambda j: hs.at[j], lambda j, s: hs.at[j, s]))
-    deal_u = deal(wu_ref, 384, tc, td)
+    run(direct_gather(cm, 'x', lambda j: hs.at[j]))
+    deal_u = deal(wu_ref, 384)
     next(deal_u)
     total = jnp.zeros((48, 1), F32)
     for d in range(8):
@@ -334,7 +339,7 @@
     def part_b(j):
         acc_b[:, rows48(j)] = jnp.dot(mb[:, rows48(j, align=16)].reshape(192, 1536), w_gu[1536:3072], preferred_element_type=F32).reshape(4, 48, 768)
 
-    run(plane_gather(cm, ma, 0, 768, part_a), plane_gather(cm, mb, 1, 768, part_b), deal_u)
+    run(deal_u, plane_gather(cm, ma, 0, part_a), plane_gather(cm, mb, 1, part_b))
 
     def hidden(j):
         s = acc_a[j] + acc_b[j]
@@ -362,10 +367,10 @@
         v = a_buf[j]
         pc[j] = jnp.dot(v, wd[0], preferred_element_type=F32)
         pd[j] = jnp.dot(v, wd[1], preferred_element_type=F32)
-    run(plane_scatter(cm, pc, 0, rx2[:8]), plane_scatter(cm, pd, 1, rx2[8:]))
+    run(plane_scatter(cm, pc, 0, rx2[:7]), plane_scatter(cm, pd, 1, rx2[7:]))
     u_buf[0, z, rows48(y, align=16)] = (hs[x, 0].astype(F32) + pc[z, rows48(y)]).astype(BF)
     u_buf[1, z, rows48(y, align=16)] = (hs[x, 1].astype(F32) + pd[z, rows48(y)]).astype(BF)
-    run(plane_gather(cm, u_buf.at[0], 0, 256, None, (False, False)), plane_gather(cm, u_buf.at[1], 1, 256, None, (False, False)))
+    run(plane_gather(cm, u_buf.at[0], 0), plane_gather(cm, u_buf.at[1], 1))
     c_v = cm.send(u_buf.at[1 - c], v_out, dev_o)
     u_out[...] = u_buf[c]
     cm.wait(c_v)
@@ -451,7 +456,7 @@
         q_sum, k_sum, v_sum, gain_all = call(
             qkv_kernel,
             (sds((192, 256), F32),) * 3 + (sds((8, 8, 128), F32),),
-            [V((8, 3, 384, 256), BF), V((2, 4, 4, 48, 384), BF), V((8, 192, 384), BF), V((8, 128), F32), V((8192, 128), BF)],
+            [V((8, 3, 384, 256), BF), V((2, 4, 4, 4, 16, 384), BF), V((8, 192, 384), BF), V((8, 128), F32), V((8192, 128), BF)],
             60, 0, 2 * 10**9, 'hhhhvv',
             resid_in, w_q, w_k, w_v, norm_attn.reshape(3, 128), norm_mlp.reshape(3, 128))
         heads = lambda a: a.reshape(192, 1, 256)
@@ -464,7 +469,7 @@
             (sds((4, 192, 384), BF), sds((4, 192, 384), BF)),
             [V((4, 192, 256), BF), V((2, 256, 384), BF), V((48, 384), BF), V((2, 1536, 384), BF)]
             + [V((4, 192, 384), F32)] * 4 + [V((4, 2, 48, 384), BF)] + [V((4, 192, 1536), BF)] * 2 + [V((4, 192, 768), F32)] * 2
-            + [V((3072, 768), BF)] + [V((192, 384), BF)] * 4 + [V((4, 192, 1536), BF), V((2, 4, 192, 384), BF), V((16384, 128), BF)]
+            + [V((3072, 768), BF), V((4, 192, 1536), BF), V((2, 4, 192, 384), BF), V((16384, 128), BF)]
             + scatter_scratch() + scatter_scratch(),
             170, 1, 7 * 10**9, 'vvvhhhv',
             attn_out.reshape(192, 256), resid_in, w_o, w_gate, w_up, w_down, gain_all)

time: 170 us -> 164 us (0.965)
  Pallas kernels: 162 us -> 156 us
    pallas_call x1, Pallas kernels: 125 us -> 119 us  [call2(): pl.pallas_call(body, out_shape=outs[0] if single else outs, in_specs=[ANY...]
where the time goes in v1:
time: 164 us; the launch traced here: 163 us
  Pallas kernels  156 us (95%)
  other arithmetic  4.81 us (3%)
    pallas_call x1, Pallas kernels, call2(): pl.pallas_call(body, out_shape=outs[0] if single else outs, in_specs=[ANY...  119 us
    pallas_call x1, Pallas kernels, call(): pl.pallas_call(body, out_shape=outs[0] if single else outs, in_specs=[ANY...  34.4 us

profile of v1, /device:TPU:1, one launch (start us, length us, event | category | flops | bytes accessed | tf_op | source)
XLA Modules:
  0.0 163.3 jit_solution(1595932591499743431)
XLA Ops:
  0.6 0.8 fusion.30
  1.4 0.1 iota_compare_fusion
  1.5 0.0 copy-start.1
  1.5 0.0 copy-start.2
  1.6 34.4 %shard_map.148 = (f32[192,256]{1,0:T(8,128)}, f32[192,256]{1,0:T(8,128)}, f32[192,256]{1,0:T(8,128)}, f32[8,8,128]{2,1,0:T(8,128)}) custom-call(bf16[1536,384]{1,0:T(8,128)(2,1)} %x_ref.3, bf16[384,256]{1,0:T(8,128)(2,1)} %wq_ref.1, bf16[384,256]{1,0:T(8,128)(2,1)} %wk_ref.1, bf16[384,256]{1,0:T(8,128)(2,1)} %wv_ref.1, bf16[3,128]{1,0:T(4,128)(2,1)} %bitcast.33, ...), custom_call_target="tpu_custom_call" | custom-call | flops 2000000000 | bytes 8000000 | tf_op jit(solution)/shard_map/pallas_call | solution.py:413
  36.0 1.5 fusion.15
  37.5 0.9 convert_element_type.32
  38.5 0.0 copy-done.1
  38.5 0.0 copy-done.2
  38.5 0.9 broadcast_select_fusion.1
  39.4 0.0 copy-start
  39.4 0.0 copy-start.3
  39.4 0.5 fusion.2
  39.9 0.2 fusion.25
  40.1 0.2 fusion.26
  40.3 0.2 fusion.27
  40.5 0.4 fusion
  40.8 0.0 copy-done
  40.9 0.2 copy-done.3
  41.0 0.7 copy.25
  41.7 119.3 %shard_map.149 = (bf16[4,192,384]{2,1,0:T(8,128)(2,1)}, bf16[4,192,384]{2,1,0:T(8,128)(2,1)}) custom-call(bf16[192,256]{1,0:T(8,128)(2,1)} %bitcast.32, bf16[1536,384]{1,0:T(8,128)(2,1)} %x_ref.3, bf16[256,384]{1,0:T(8,128)(2,1)} %wo_ref.1, bf16[384,1536]{1,0:T(8,128)(2,1)} %wg_ref.1, bf16[384,1536]{1,0:T(8,128)(2,1)} %wu_ref.1, bf16[1536,384]{1,0:T(8,128)(2,1)} %wd_ref.1, ...), custom_call_target="tpu_custom_call" | custom-call | flops 7000000000 | bytes 8000000 | tf_op jit(solution)/shard_map/pallas_call | solution.py:426
  161.0 2.4 %shard_map.150 = bf16[1536,384]{1,0:T(8,128)(2,1)} custom-call(bf16[4,192,384]{2,1,0:T(8,128)(2,1)} %get-tuple-element.13.u_ref, bf16[4,192,384]{2,1,0:T(8,128)(2,1)} %get-tuple-element.14.v_ref), custom_call_target="tpu_custom_call" | custom-call | tf_op jit(solution)/shard_map/pallas_call | solution.py:476
  (3 shorter events, 0.0 us)
Async XLA Ops:
  1.5 36.9 %copy-start.1 = (bf16[192,1,16,256]{3,2,1,0:T(8,128)(2,1)S(1)}, bf16[192,1,16,256]{3,2,1,0:T(8,128)(2,1)}, u32[]{:S(2)}) copy-start(bf16[192,1,16,256]{3,2,1,0:T(8,128)(2,1)} %param.14) | copy-start | bytes 4718596
  1.5 36.9 %copy-start.2 = (bf16[192,1,16,256]{3,2,1,0:T(8,128)(2,1)S(1)}, bf16[192,1,16,256]{3,2,1,0:T(8,128)(2,1)}, u32[]{:S(2)}) copy-start(bf16[192,1,16,256]{3,2,1,0:T(8,128)(2,1)} %param.15) | copy-start | bytes 4718596
  39.4 1.5 copy-start
  39.4 1.7 %copy-start.3 = (bf16[192,1,16,256]{3,2,1,0:T(8,128)(2,1)}, bf16[192,1,16,256]{3,2,1,0:T(8,128)(2,1)S(1)}, u32[]{:S(2)}) copy-start(bf16[192,1,16,256]{3,2,1,0:T(8,128)(2,1)S(1)} %get-tuple-element.21) | copy-start | bytes 4718596

commit v2 on v1

--- a/solution.py
+++ b/solution.py
@@ -2,6 +2,7 @@
 
 import jax
 import jax.numpy as jnp
+import numpy as np
 from jax import lax
 from jax.experimental import pallas as pl
 from jax.experimental.pallas import tpu as pltpu
@@ -189,7 +190,7 @@
     return jnp.concatenate([g[3 * k + j:3 * k + j + 1] for j in range(3)], axis=1)
 
 
-def qkv_kernel(x_ref, wq_ref, wk_ref, wv_ref, ga_ref, gm_ref, q_ref, k_ref, v_ref, g_ref, w_buf, xg, n_buf, gain_buf, wait_buf, *sems):
+def qkv_kernel(x_ref, wq_ref, wk_ref, wv_ref, ga_ref, gm_ref, qkv_ref, g_ref, w_buf, xg, n_buf, gain_buf, wait_buf, *sems):
     cm = Comm(wait_buf, sems)
     x, c, dm = cm.x, cm.c, cm.dm
     peers = [cm.tp * 8 + lax.rem(dm + k, 8) for k in range(1, 8)]
@@ -245,12 +246,10 @@
     for d in range(8):
         v = xg[d % 2, :, 0:3, d // 2].reshape(192, 384).astype(F32)
         n_buf[d] = (v * inv * (1.0 + gain_row(g_ref, d, 0))).astype(BF)
-    outs = (q_ref, k_ref, v_ref)
-
     def add(j, first=False):
-        for n, out in enumerate(outs):
+        for n in range(3):
             part = jnp.dot(n_buf[j * 2], w_buf[j * 2, n], preferred_element_type=F32) + jnp.dot(n_buf[j * 2 + 1], w_buf[j * 2 + 1, n], preferred_element_type=F32)
-            out[...] = part if first else out[...] + part
+            qkv_ref[n] = part if first else qkv_ref[n] + part
 
     cm.wait(*e, *mine)
     add(i, True)
@@ -377,59 +376,80 @@
     cm.drain()
 
 
-def rope_rotate(vectors, positions):
-    half_dim = vectors.shape[-1] // 2
-    inv_freq = ROPE_THETA ** (-2.0 * jnp.arange(half_dim, dtype=jnp.float32) / vectors.shape[-1])
-    angles = positions.astype(jnp.float32)[:, None] * inv_freq[None, :]
-    cos_part = jnp.cos(angles)[:, None, :]
-    sin_part = jnp.sin(angles)[:, None, :]
-    first_half = vectors[..., :half_dim]
-    second_half = vectors[..., half_dim:]
-    return jnp.concatenate([first_half * cos_part - second_half * sin_part, second_half * cos_part + first_half * sin_part], axis=-1)
-
-
-def attend(q_rot, k_cache, v_cache, k_new, v_new, lengths):
-    slot_ids = jnp.arange(k_cache.shape[2])
-    slot_hit = slot_ids[None, :] == lengths[:, None]
-    valid_mask = slot_ids[None, :] <= lengths[:, None]
-    k_upd = jnp.where(slot_hit[:, None, :, None], k_new[:, :, None, :], k_cache)
-    v_upd = jnp.where(slot_hit[:, None, :, None], v_new[:, :, None, :], v_cache)
-    scores = jnp.einsum('bhe,bhte->bht', q_rot, k_upd, preferred_element_type=jnp.float32)
-    scores = jnp.where(valid_mask[:, None, :], scores, -1e30)
-    attn_probs = jax.nn.softmax(scores, axis=-1).astype(jnp.bfloat16)
-    attn_out = jnp.einsum('bht,bhte->bhe', attn_probs, v_upd, preferred_element_type=jnp.float32)
-    return attn_out.astype(jnp.bfloat16), k_upd, v_upd
+def rope_table():
+    inv_freq = np.float32(ROPE_THETA) ** (np.float32(-2.0) * np.arange(128, dtype=np.float32) / np.float32(256))
+    angles = np.arange(16, dtype=np.float32)[:, None] * inv_freq[None, :].astype(np.float32)
+    return np.stack([np.cos(angles), np.sin(angles)]).astype(np.float32)
+
+
+def attend_kernel(qkv_ref, kc_ref, vc_ref, len_ref, tab_ref, o_ref, ku_ref, vu_ref):
+    step = o_ref.shape[0]
+    at = pl.ds(pl.multiple_of(pl.program_id(0) * step, step), step)
+    pos = len_ref[at, :]
+    cos = jnp.zeros((step, 128), F32)
+    sin = jnp.zeros((step, 128), F32)
+    for t in range(16):
+        cos = jnp.where(pos == t, tab_ref[0, t:t + 1], cos)
+        sin = jnp.where(pos == t, tab_ref[1, t:t + 1], sin)
+
+    def rope(n):
+        lo, hi = qkv_ref[n, at, 0:128], qkv_ref[n, at, 128:256]
+        return lo * cos - hi * sin, hi * cos + lo * sin
+
+    tall = lambda a: a.reshape(step, 1, 128)
+    rounded = lambda a: a.astype(BF).astype(F32)
+    q = [tall(rounded(a * 256 ** -0.5)) for a in rope(0)]
+    k_new = [tall(rounded(a)) for a in rope(1)]
+    v_new = [tall(rounded(qkv_ref[2, at, 128 * n:128 * n + 128])) for n in range(2)]
+    slot = lax.broadcasted_iota(jnp.int32, (step, 16, 128), 1)
+    pos3 = pos.reshape(step, 1, 128)
+    hit = slot == pos3
+    prod = None
+    for n in range(2):
+        lanes = slice(128 * n, 128 * n + 128)
+        k = jnp.where(hit, k_new[n], kc_ref[at, :, lanes].astype(F32))
+        ku_ref[:, :, lanes] = k.astype(BF)
+        prod = k * q[n] if prod is None else prod + k * q[n]
+    score = jnp.sum(prod, axis=2, keepdims=True)
+    valid = (slot <= pos3)[:, :, 0:1]
+    score = jnp.where(valid, score, -1e30)
+    e = jnp.exp(score - jnp.max(score, axis=1, keepdims=True))
+    p = rounded(e / jnp.sum(e, axis=1, keepdims=True))
+    for n in range(2):
+        lanes = slice(128 * n, 128 * n + 128)
+        v = jnp.where(hit, v_new[n], vc_ref[at, :, lanes].astype(F32))
+        vu_ref[:, :, lanes] = v.astype(BF)
+        o_ref[:, lanes] = jnp.sum(jnp.where(slot <= pos3, p * v, 0.0), axis=1).astype(BF)
 
 
 VM = pl.BlockSpec(memory_space=pltpu.VMEM)
-VMEM_LIMIT = 60 * 1024 * 1024
-
-
-ANY = pl.BlockSpec(memory_space=pl.ANY)
-
-
-def call(body, outs, scratch, sems, cid, flops, where, *args):
+
+
+HB = pl.BlockSpec(memory_space=pltpu.HBM)
+
+
+def call(body, outs, scratch, sems, cid, limit, flops, where, *args):
     single = len(outs) == 1
     return pl.pallas_call(
         body,
         out_shape=outs[0] if single else outs,
-        in_specs=[ANY if w == 'h' else VM for w in where],
+        in_specs=[HB if w == 'h' else VM for w in where],
         out_specs=VM if single else [VM] * len(outs),
         scratch_shapes=scratch + [pltpu.SemaphoreType.DMA] * sems,
-        compiler_params=pltpu.CompilerParams(collective_id=cid, has_side_effects=True, vmem_limit_bytes=VMEM_LIMIT),
+        compiler_params=pltpu.CompilerParams(collective_id=cid, has_side_effects=True, vmem_limit_bytes=limit * 2**20),
         cost_estimate=pl.CostEstimate(flops=flops, bytes_accessed=8_000_000, transcendentals=0),
     )(*args)
 
 
-def call2(body, outs, scratch, sems, cid, flops, where, *args):
+def call2(body, outs, scratch, sems, cid, limit, flops, where, *args):
     single = len(outs) == 1
     return pl.pallas_call(
         body,
         out_shape=outs[0] if single else outs,
-        in_specs=[ANY if w == 'h' else VM for w in where],
+        in_specs=[HB if w == 'h' else VM for w in where],
         out_specs=VM if single else [VM] * len(outs),
         scratch_shapes=scratch + [pltpu.SemaphoreType.DMA] * sems,
-        compiler_params=pltpu.CompilerParams(collective_id=cid, has_side_effects=True, vmem_limit_bytes=VMEM_LIMIT),
+        compiler_params=pltpu.CompilerParams(collective_id=cid, has_side_effects=True, vmem_limit_bytes=limit * 2**20),
         cost_estimate=pl.CostEstimate(flops=flops, bytes_accessed=8_000_000, transcendentals=0),
     )(*args)
 
@@ -452,18 +472,20 @@
     V = pltpu.VMEM
 
     def local_step(resid_in, k_cache, v_cache, cache_len, norm_attn, w_q, w_k, w_v, w_o, norm_mlp, w_gate, w_up, w_down):
+        qkv, gain_all = call(
+            qkv_kernel,
+            (sds((3, 192, 256), F32), sds((8, 8, 128), F32)),
+            [V((8, 3, 384, 256), BF), V((2, 4, 4, 4, 16, 384), BF), V((8, 192, 384), BF), V((8, 128), F32), V((8192, 128), BF)],
+            60, 0, 58, 2 * 10**9, 'hhhhvv',
+            resid_in, w_q, w_k, w_v, norm_attn.reshape(3, 128), norm_mlp.reshape(3, 128))
         lengths = lax.dynamic_slice_in_dim(cache_len, lax.axis_index('dm') * 192, 192)
-        q_sum, k_sum, v_sum, gain_all = call(
-            qkv_kernel,
-            (sds((192, 256), F32),) * 3 + (sds((8, 8, 128), F32),),
-            [V((8, 3, 384, 256), BF), V((2, 4, 4, 4, 16, 384), BF), V((8, 192, 384), BF), V((8, 128), F32), V((8192, 128), BF)],
-            60, 0, 2 * 10**9, 'hhhhvv',
-            resid_in, w_q, w_k, w_v, norm_attn.reshape(3, 128), norm_mlp.reshape(3, 128))
-        heads = lambda a: a.reshape(192, 1, 256)
-        q_rot = (rope_rotate(heads(q_sum), lengths) * 256 ** -0.5).astype(BF)
-        k_new = rope_rotate(heads(k_sum), lengths).astype(BF)
-        v_new = heads(v_sum).astype(BF)
-        attn_out, k_upd, v_upd = attend(q_rot, k_cache, v_cache, k_new, v_new, lengths)
+        cache, step = sds((192, 16, 256), BF), 48
+        attn_out, k_upd, v_upd = pl.pallas_call(
+            attend_kernel, name='attend', out_shape=(sds((192, 256), BF), cache, cache), grid=(192 // step,), in_specs=[VM] * 5,
+            out_specs=[pl.BlockSpec((step, 256), lambda b: (b, 0))] + [pl.BlockSpec((step, 16, 256), lambda b: (b, 0, 0))] * 2,
+            compiler_params=pltpu.CompilerParams(vmem_limit_bytes=20 * 2**20),
+        )(qkv, k_cache.reshape(192, 16, 256), v_cache.reshape(192, 16, 256), jnp.broadcast_to(lengths[:, None], (192, 128)), jnp.asarray(rope_table()))
+        k_upd, v_upd = k_upd.reshape(192, 1, 16, 256), v_upd.reshape(192, 1, 16, 256)
         mine, theirs = call2(
             post_kernel,
             (sds((4, 192, 384), BF), sds((4, 192, 384), BF)),
@@ -471,9 +493,9 @@
             + [V((4, 192, 384), F32)] * 4 + [V((4, 2, 48, 384), BF)] + [V((4, 192, 1536), BF)] * 2 + [V((4, 192, 768), F32)] * 2
             + [V((3072, 768), BF), V((4, 192, 1536), BF), V((2, 4, 192, 384), BF), V((16384, 128), BF)]
             + scatter_scratch() + scatter_scratch(),
-            170, 1, 7 * 10**9, 'vvvhhhv',
-            attn_out.reshape(192, 256), resid_in, w_o, w_gate, w_up, w_down, gain_all)
-        resid_out = pl.pallas_call(join_kernel, out_shape=sds((1536, 384), BF), in_specs=[VM, VM], out_specs=VM)(mine, theirs)
+            170, 1, 44, 7 * 10**9, 'vvvhhhv',
+            attn_out, resid_in, w_o, w_gate, w_up, w_down, gain_all)
+        resid_out = pl.pallas_call(join_kernel, out_shape=sds((1536, 384), BF), in_specs=[VM, VM], out_specs=VM, compiler_params=pltpu.CompilerParams(vmem_limit_bytes=8 * 2**20))(mine, theirs)
         return resid_out, k_upd, v_upd
 
     return jax.shard_map(local_step, mesh=mesh, in_specs=in_specs, out_specs=out_specs, check_vma=False)

time: 164 us -> 160 us (0.976)
  other arithmetic: 4.81 us -> 0 us
    pallas_call x2 -> x3, Pallas kernels: 154 us -> 156 us  [the longest x1 117 us: call2(): pl.pallas_call(body, out_shape=outs[0] if single else outs, in_specs=[HB...]
    convert_element_type x4 -> x0, other arithmetic: 1.89 us -> none  [the longest x1 0.94 us: local_step(): v_new = heads(v_sum).astype(BF)]
where the time goes in v2:
time: 160 us
  Pallas kernels  157 us (98%)
  local copies, waits for them, and re-layouts  1.96 us (1%)
    pallas_call x1, Pallas kernels, call2(): pl.pallas_call(body, out_shape=outs[0] if single else outs, in_specs=[HB...  117 us
    pallas_call x1, Pallas kernels, call(): pl.pallas_call(body, out_shape=outs[0] if single else outs, in_specs=[HB...  34.4 us
    pallas_call x1, Pallas kernels, local_step(): pl.pallas_call(attend_kernel, name='attend', out_shape=(sds((192, 256), B...  4.36 us

profile of v2, /device:TPU:1, one launch (start us, length us, event | category | flops | bytes accessed | tf_op | source)
XLA Modules:
  0.0 159.8 jit_solution(202769311249310982)
XLA Ops:
  0.6 0.8 dynamic_slice.3
  1.4 0.1 broadcast_in_dim.2.len_ref
  1.5 0.0 copy-start
  1.5 0.0 copy-start.1
  1.5 0.0 copy-start.3
  1.5 0.0 copy-start.7
  1.5 34.4 %shard_map.157 = (f32[3,192,256]{2,1,0:T(8,128)}, f32[8,8,128]{2,1,0:T(8,128)}) custom-call(bf16[1536,384]{1,0:T(8,128)(2,1)} %x_ref.3, bf16[384,256]{1,0:T(8,128)(2,1)} %wq_ref.1, bf16[384,256]{1,0:T(8,128)(2,1)} %wk_ref.1, bf16[384,256]{1,0:T(8,128)(2,1)} %wv_ref.1, bf16[3,128]{1,0:T(4,128)(2,1)} %bitcast.14, bf16[3,128]{1,0:T(4,128)(2,1)} %bitcast.15), custom_call_target="tpu_custom_call" | custom-call | flops 2000000000 | bytes 8000000 | tf_op jit(solution)/shard_map/pallas_call | solution.py:433
  36.0 0.0 copy-done
  36.0 0.0 copy-done.1
  36.0 0.0 copy-done.3
  36.0 0.0 copy-start.2
  36.0 1.1 copy-done.2
  37.1 0.0 copy-start.4
  37.1 0.0 copy-start.5
  37.1 0.0 copy-start.6
  37.1 0.0 copy-start.8
  37.1 0.0 copy-start.9
  37.1 4.4 %attend.1 = (bf16[192,256]{1,0:T(8,128)(2,1)S(1)}, bf16[192,16,256]{2,1,0:T(8,128)(2,1)}, bf16[192,16,256]{2,1,0:T(8,128)(2,1)}) custom-call(f32[3,192,256]{2,1,0:T(8,128)S(1)} %copy-done.2, bf16[192,16,256]{2,1,0:T(8,128)(2,1)S(1)} %bitcast.10, bf16[192,16,256]{2,1,0:T(8,128)(2,1)S(1)} %bitcast.11, s32[192,128]{1,0:T(8,128)S(1)} %broadcast_in_dim.2.len_ref, ...), custom_call_target="tpu_custom_call" | custom-call | tf_op jit(solution)/shard_map/attend/pallas_call | solution.py:483
  41.4 0.0 copy-done.7
  41.4 0.0 copy-done.4
  41.5 0.0 copy-done.5
  41.5 0.0 copy-done.6
  41.5 0.0 copy-done.8
  41.5 0.0 copy-done.9
  41.5 117.2 %shard_map.158 = (bf16[4,192,384]{2,1,0:T(8,128)(2,1)S(1)}, bf16[4,192,384]{2,1,0:T(8,128)(2,1)S(1)}) custom-call(bf16[192,256]{1,0:T(8,128)(2,1)S(1)} %get-tuple-element.11.o_ref, bf16[1536,384]{1,0:T(8,128)(2,1)S(1)} %copy-done.4, bf16[256,384]{1,0:T(8,128)(2,1)S(1)} %copy-done.8, bf16[384,1536]{1,0:T(8,128)(2,1)S(1)} %copy-done.5, ...), custom_call_target="tpu_custom_call" | custom-call | flops 7000000000 | bytes 8000000 | tf_op jit(solution)/shard_map/pallas_call | solution.py:446
  158.6 1.1 shard_map.159
Async XLA Ops:
  1.5 34.5 %copy-start = (bf16[192,1,16,256]{3,2,1,0:T(8,128)(2,1)S(1)}, bf16[192,1,16,256]{3,2,1,0:T(8,128)(2,1)}, u32[]{:S(2)}) copy-start(bf16[192,1,16,256]{3,2,1,0:T(8,128)(2,1)} %param.15) | copy-start | bytes 4718596
  1.5 34.5 %copy-start.1 = (bf16[192,1,16,256]{3,2,1,0:T(8,128)(2,1)S(1)}, bf16[192,1,16,256]{3,2,1,0:T(8,128)(2,1)}, u32[]{:S(2)}) copy-start(bf16[192,1,16,256]{3,2,1,0:T(8,128)(2,1)} %param.16) | copy-start | bytes 4718596
  1.5 34.5 %copy-start.3 = (f32[2,16,128]{2,1,0:T(8,128)S(1)}, f32[2,16,128]{2,1,0:T(8,128)}, u32[]{:S(2)}) copy-start(f32[2,16,128]{2,1,0:T(8,128)} %constant.12.clone.tab_ref) | copy-start | bytes 49156
  1.5 39.9 %copy-start.7 = (bf16[1536,384]{1,0:T(8,128)(2,1)S(1)}, bf16[1536,384]{1,0:T(8,128)(2,1)}, u32[]{:S(2)}) copy-start(bf16[1536,384]{1,0:T(8,128)(2,1)} %wd_ref.1) | copy-start | bytes 3538948
  36.0 1.1 copy-start.2
  37.1 4.4 %copy-start.4 = (bf16[1536,384]{1,0:T(8,128)(2,1)S(1)}, bf16[1536,384]{1,0:T(8,128)(2,1)}, u32[]{:S(2)}) copy-start(bf16[1536,384]{1,0:T(8,128)(2,1)} %x_ref.3) | copy-start | bytes 3538948
  37.1 4.4 %copy-start.5 = (bf16[384,1536]{1,0:T(8,128)(2,1)S(1)}, bf16[384,1536]{1,0:T(8,128)(2,1)}, u32[]{:S(2)}) copy-start(bf16[384,1536]{1,0:T(8,128)(2,1)} %wg_ref.1) | copy-start | bytes 3538948
  37.1 4.4 %copy-start.6 = (bf16[384,1536]{1,0:T(8,128)(2,1)S(1)}, bf16[384,1536]{1,0:T(8,128)(2,1)}, u32[]{:S(2)}) copy-start(bf16[384,1536]{1,0:T(8,128)(2,1)} %wu_ref.1) | copy-start | bytes 3538948
  37.1 4.4 %copy-start.8 = (bf16[256,384]{1,0:T(8,128)(2,1)S(1)}, bf16[256,384]{1,0:T(8,128)(2,1)}, u32[]{:S(2)}) copy-start(bf16[256,384]{1,0:T(8,128)(2,1)} %wo_ref.1) | copy-start | bytes 589828
  37.1 4.4 %copy-start.9 = (f32[8,8,128]{2,1,0:T(8,128)S(1)}, f32[8,8,128]{2,1,0:T(8,128)}, u32[]{:S(2)}) copy-start(f32[8,8,128]{2,1,0:T(8,128)} %get-tuple-element.12.g_ref) | copy-start | bytes 98308

commit v3 on v2

--- a/solution.py
+++ b/solution.py
@@ -39,17 +39,20 @@
             pl.semaphore_signal(sem, inc=1, device_id=dev, device_id_type=LOGICAL)
         pl.semaphore_wait(sem, len(peers))
 
-    def send(self, src, dst, dev):
+    def send(self, src, dst, dev, recv=None):
         rows = math.prod(dst.shape) * dst.dtype.itemsize // 256
         if not self.groups or self.groups[-1][1] + rows > self.wait_buf.shape[0]:
             self.groups.append([self.sems.pop(), 0])
         self.groups[-1][1] += rows
-        recv = self.sems.pop()
+        recv = self.sems.pop() if recv is None else recv
         pltpu.make_async_remote_copy(src_ref=src, dst_ref=dst, send_sem=self.groups[-1][0], recv_sem=recv, device_id=dev, device_id_type=LOGICAL).start()
         return recv, rows
 
     def wait(self, *copies):
+        total = {}
         for sem, rows in copies:
+            total[id(sem)] = sem, total.get(id(sem), (sem, 0))[1] + rows
+        for sem, rows in total.values():
             part = self.wait_buf.at[0:rows]
             pltpu.make_async_copy(part, part, sem).wait()
 
@@ -60,6 +63,7 @@
         return sem, rows
 
     def drain(self):
+        assert not self.sems, len(self.sems)
         self.wait(*self.groups)
 
 
@@ -79,7 +83,7 @@
         a0 = cm.send(hf(i, 0), hf(i, 0), dr)
         b1 = cm.send(hf(i, 1), hf(i, 1), dl)
         a1 = cm.send(hf(i, 1), hf(i, 1), dr)
-        b0 = cm.send(hf(i, 0), hf(i, 0), dl)
+        b0 = cm.send(hf(i, 0), hf(i, 0), dl, a1[0])
         late = (a1, b0)
     else:
         a0 = cm.send(blk(i), blk(i), dr)
@@ -89,27 +93,27 @@
     cm.wait(a0)
     c = cm.send(hf(l, 0), hf(l, 0), dr)
     cm.wait(b1)
-    d = cm.send(hf(r, 1), hf(r, 1), dl)
+    d = cm.send(hf(r, 1), hf(r, 1), dl, c[0])
     yield
     cm.wait(*late)
     yield
     cm.wait(c, d)
 
 
-def direct4(cm, axis, src, dst):
+def direct4(cm, axis, src, dst, recv=None):
     (i, r, o, l), dr, dl = cm.rings[axis]
-    return [cm.send(src(o), dst(1), cm.opposite[axis]), cm.send(src(r), dst(0), dr), cm.send(src(l), dst(2), dl)]
+    return [cm.send(src(o), dst(1), cm.opposite[axis], recv), cm.send(src(r), dst(0), dr, recv), cm.send(src(l), dst(2), dl, recv)]
 
 
 def direct_gather(cm, axis, blk):
     own = blk(cm.rings[axis][0][0])
-    cps = direct4(cm, axis, lambda j: own, lambda k: own)
+    cps = direct4(cm, axis, lambda j: own, lambda k: own, cm.sems.pop())
     yield
     cm.wait(*cps)
 
 
 def direct_scatter(cm, axis, blk, rx):
-    cps = direct4(cm, axis, blk, lambda k: rx[k])
+    cps = direct4(cm, axis, blk, lambda k: rx[k], cm.sems.pop())
     yield
     cm.wait(*cps)
     blk(cm.rings[axis][0][0])[...] += (rx[0][...] + rx[2][...]) + rx[1][...]
@@ -121,14 +125,14 @@
     c0 = cm.send(hf(o, 0), ro0, dr)
     c1 = cm.send(hf(o, 1), ro1, dl)
     c2 = cm.send(hf(r, 1), hrx(rl, 1), dr)
-    c3 = cm.send(hf(l, 0), hrx(rr, 0), dl)
+    c3 = cm.send(hf(l, 0), hrx(rr, 0), dl, c2[0])
     yield
     cm.wait(c0)
     hf(r, 0)[...] += ro0[...]
-    c4 = cm.send(hf(r, 0), hrx(rl, 0), dr)
+    c4 = cm.send(hf(r, 0), hrx(rl, 0), dr, c2[0])
     cm.wait(c1)
     hf(l, 1)[...] += ro1[...]
-    c5 = cm.send(hf(l, 1), hrx(rr, 1), dl)
+    c5 = cm.send(hf(l, 1), hrx(rr, 1), dl, c2[0])
     yield
     cm.wait(c2, c3, c4, c5)
     blk(i)[...] += rl[...] + rr[...]
@@ -155,33 +159,59 @@
     return [V((2, 48, 384), F32)] * 2 + [V((4, 48, 384), F32)] * 2 + small + [V((96, 384), F32)] * 2 + [V((192, 384), F32)] * 2 + small
 
 
-def plane_gather(cm, m, h, near=None):
+def plane_gather(cm, m, h):
     at = lambda j: rows48(j, align=16)
     if h == 0:
-        second = 'z'
         yield from direct_gather(cm, 'y', lambda j: m.at[cm.z, at(j)])
-        big, bigh = (lambda j: m.at[j]), (lambda j, s: m.at[j, 96 * s:96 * s + 96])
+        yield from direct_gather(cm, 'z', lambda j: m.at[j])
     else:
-        second = 'y'
         yield from direct_gather(cm, 'z', lambda j: m.at[j, at(cm.y)])
-        big, bigh = (lambda j: m.at[:, at(j)]), (lambda j, s: m.at[2 * s:2 * s + 2, at(j)])
-    if near is None:
-        yield from direct_gather(cm, second, big)
-        return
-    i, r, o, l = cm.rings[second][0]
-    g = gather4(cm, second, big, bigh)
-    next(g)
-    yield
-    next(g)
+        yield from direct_gather(cm, 'y', lambda j: m.at[:, at(j)])
+
+
+def plane_stream(cm, m, h, near):
+    at = lambda j: rows48(j, align=16)
+    first, second = ('y', 'z') if h == 0 else ('z', 'y')
+    piece = (lambda b, k: m.at[b, at(k)]) if h == 0 else (lambda b, k: m.at[k, at(b)])
+    ki, kr, ko, kl = cm.rings[first][0]
+    (i, r, o, l), dr, dl = cm.rings[second]
+    right, left = {}, {}
+
+    def out(name, k):
+        right[name] = cm.send(piece(i, k), piece(i, k), dr)
+        left[name] = cm.send(piece(i, k), piece(i, k), dl)
+
+    small = direct4(cm, first, lambda j: piece(i, ki), lambda k: piece(i, ki))
+    yield
+    out('i', ki)
+    yield
+    cm.wait(small[1])
+    out('l', kl)
+    cm.wait(small[2])
+    out('r', kr)
+    yield
+    cm.wait(small[0])
+    out('o', ko)
+    yield
+    cm.wait(right['i'])
+    fr = [cm.send(piece(l, ki), piece(l, ki), dr)]
+    cm.wait(left['i'])
     yield
     near(i)
     yield
-    next(g)
+    cm.wait(right['l'])
+    fr.append(cm.send(piece(l, kl), piece(l, kl), dr, fr[0][0]))
+    cm.wait(left['l'], left['r'])
+    fl = [cm.send(piece(r, kr), piece(r, kr), dl)]
+    yield
+    cm.wait(left['o'])
+    fl.append(cm.send(piece(r, ko), piece(r, ko), dl, fl[0][0]))
+    cm.wait(right['r'], right['o'])
+    yield
     near(l)
     near(r)
     yield
-    for _ in g:
-        pass
+    cm.wait(*fr, *fl)
     near(o)
 
 
@@ -200,7 +230,8 @@
     second = jnp.where(c == 0, cm.z, cm.y)
     start = first * 48 + jnp.minimum(second, 2) * 16
     piece = lambda d: x_ref.at[pl.ds(pl.multiple_of(d * 192 + start, 16), 16), :]
-    xs = [cm.send(piece(lax.rem(dm + k + 1, 8)), xg.at[c, first, second, x], dev) for k, dev in enumerate(peers)]
+    together = cm.sems.pop()
+    xs = [cm.send(piece(lax.rem(dm + k + 1, 8)), xg.at[c, first, second, x], dev, together) for k, dev in enumerate(peers)]
     gain_buf[0:3] = ga_ref[...].astype(F32)
     gain_buf[3:6] = gm_ref[...].astype(F32)
     gain_buf[6:8] = jnp.zeros((2, 128), F32)
@@ -213,7 +244,8 @@
     a = [cm.send(ws[n].at[p], rows(i).at[n, p], dr) for n, p in pieces]
     b = [cm.send(ws[n].at[p], rows(i).at[n, p], dl) for n, p in pieces[::-1]]
     e = [cm.send(w, rows(i).at[n], dev_o) for n, w in enumerate(ws)]
-    gs = [cm.send(gain_buf, g_ref.at[dm], dev) for dev in peers]
+    together = cm.sems.pop()
+    gs = [cm.send(gain_buf, g_ref.at[dm], dev, together) for dev in peers]
     mine = [cm.local(w, w_buf.at[dm, n]) for n, w in enumerate(ws)]
     xs.append(cm.local(piece(dm), xg.at[c, first, second, x]))
     g_ref[dm] = gain_buf[...]
@@ -287,12 +319,12 @@
     kblk = lambda j: pl.ds(pl.multiple_of((j * 2 + c) * 384, 16), 384)
     hcol = lambda j: pl.ds(pl.multiple_of(j * 384, 128), 384)
 
-    def deal(w_ref, col):
+    def deal(w_ref, col, pause):
         to = pl.ds(col, 384)
         own = w_gu.at[kblk(i), to]
         cps = direct4(cm, 'x', lambda j: w_ref.at[:, hcol(j)], lambda k: own)
         here = [cm.local(w_ref.at[:, hcol(i)], own), cm.send(w_ref.at[:, hcol(i)], own, dev_o)]
-        for _ in range(3):
+        for _ in range(pause):
             yield
         for cp, j in zip(cps[1:] + cps[:1], (l, r, o)):
             cm.wait(cp)
@@ -302,7 +334,7 @@
 
     for _ in go:
         pass
-    deal_g = deal(wg_ref, 0)
+    deal_g = deal(wg_ref, 0, 3)
     next(deal_g)
     cm.wait(c_wo)
 
@@ -321,7 +353,7 @@
     hs[x, 0] = (jnp.where(first, mine, theirs) + pa[z, rows48(y)]).astype(BF)
     hs[x, 1] = (jnp.where(first, theirs, mine) + pb[z, rows48(y)]).astype(BF)
     run(direct_gather(cm, 'x', lambda j: hs.at[j]))
-    deal_u = deal(wu_ref, 384)
+    deal_u = deal(wu_ref, 384, 5)
     next(deal_u)
     total = jnp.zeros((48, 1), F32)
     for d in range(8):
@@ -338,7 +370,7 @@
     def part_b(j):
         acc_b[:, rows48(j)] = jnp.dot(mb[:, rows48(j, align=16)].reshape(192, 1536), w_gu[1536:3072], preferred_element_type=F32).reshape(4, 48, 768)
 
-    run(deal_u, plane_gather(cm, ma, 0, part_a), plane_gather(cm, mb, 1, part_b))
+    run(deal_u, plane_stream(cm, ma, 0, part_a), plane_stream(cm, mb, 1, part_b))
 
     def hidden(j):
         s = acc_a[j] + acc_b[j]
@@ -476,7 +508,7 @@
             qkv_kernel,
             (sds((3, 192, 256), F32), sds((8, 8, 128), F32)),
             [V((8, 3, 384, 256), BF), V((2, 4, 4, 4, 16, 384), BF), V((8, 192, 384), BF), V((8, 128), F32), V((8192, 128), BF)],
-            60, 0, 58, 2 * 10**9, 'hhhhvv',
+            37, 0, 58, 2 * 10**9, 'hhhhvv',
             resid_in, w_q, w_k, w_v, norm_attn.reshape(3, 128), norm_mlp.reshape(3, 128))
         lengths = lax.dynamic_slice_in_dim(cache_len, lax.axis_index('dm') * 192, 192)
         cache, step = sds((192, 16, 256), BF), 48
@@ -493,7 +525,7 @@
             + [V((4, 192, 384), F32)] * 4 + [V((4, 2, 48, 384), BF)] + [V((4, 192, 1536), BF)] * 2 + [V((4, 192, 768), F32)] * 2
             + [V((3072, 768), BF), V((4, 192, 1536), BF), V((2, 4, 192, 384), BF), V((16384, 128), BF)]
             + scatter_scratch() + scatter_scratch(),
-            170, 1, 44, 7 * 10**9, 'vvvhhhv',
+            86, 1, 44, 7 * 10**9, 'vvvhhhv',
             attn_out, resid_in, w_o, w_gate, w_up, w_down, gain_all)
         resid_out = pl.pallas_call(join_kernel, out_shape=sds((1536, 384), BF), in_specs=[VM, VM], out_specs=VM, compiler_params=pltpu.CompilerParams(vmem_limit_bytes=8 * 2**20))(mine, theirs)
         return resid_out, k_upd, v_upd

time: 160 us -> 157 us (0.981)
  Pallas kernels: 157 us -> 154 us
    pallas_call x1, Pallas kernels: 117 us -> 115 us  [call2(): pl.pallas_call(body, out_shape=outs[0] if single else outs, in_specs=[HB...]
where the time goes in v3:
time: 157 us
  Pallas kernels  154 us (98%)
  local copies, waits for them, and re-layouts  1.96 us (1%)
    pallas_call x1, Pallas kernels, call2(): pl.pallas_call(body, out_shape=outs[0] if single else outs, in_specs=[HB...  115 us
    pallas_call x1, Pallas kernels, call(): pl.pallas_call(body, out_shape=outs[0] if single else outs, in_specs=[HB...  34.2 us
    pallas_call x1, Pallas kernels, local_step(): pl.pallas_call(attend_kernel, name='attend', out_shape=(sds((192, 256), B...  4.18 us

profile of v3, /device:TPU:1, one launch (start us, length us, event | category | flops | bytes accessed | tf_op | source)
XLA Modules:
  0.0 157.1 jit_solution(8808507353447242677)
XLA Ops:
  0.6 0.8 dynamic_slice.3
  1.4 0.1 broadcast_in_dim.2.len_ref
  1.5 0.0 copy-start
  1.5 0.0 copy-start.1
  1.5 0.0 copy-start.3
  1.5 0.0 copy-start.7
  1.5 34.2 %shard_map.157 = (f32[3,192,256]{2,1,0:T(8,128)}, f32[8,8,128]{2,1,0:T(8,128)}) custom-call(bf16[1536,384]{1,0:T(8,128)(2,1)} %x_ref.3, bf16[384,256]{1,0:T(8,128)(2,1)} %wq_ref.1, bf16[384,256]{1,0:T(8,128)(2,1)} %wk_ref.1, bf16[384,256]{1,0:T(8,128)(2,1)} %wv_ref.1, bf16[3,128]{1,0:T(4,128)(2,1)} %bitcast.14, bf16[3,128]{1,0:T(4,128)(2,1)} %bitcast.15), custom_call_target="tpu_custom_call" | custom-call | flops 2000000000 | bytes 8000000 | tf_op jit(solution)/shard_map/pallas_call | solution.py:465
  35.7 0.0 copy-done
  35.8 0.0 copy-done.1
  35.8 0.0 copy-done.3
  35.8 0.0 copy-start.2
  35.8 1.1 copy-done.2
  36.8 0.0 copy-start.4
  36.8 0.0 copy-start.5
  36.8 0.0 copy-start.6
  36.8 0.0 copy-start.8
  36.9 0.0 copy-start.9
  36.9 4.2 %attend.1 = (bf16[192,256]{1,0:T(8,128)(2,1)S(1)}, bf16[192,16,256]{2,1,0:T(8,128)(2,1)}, bf16[192,16,256]{2,1,0:T(8,128)(2,1)}) custom-call(f32[3,192,256]{2,1,0:T(8,128)S(1)} %copy-done.2, bf16[192,16,256]{2,1,0:T(8,128)(2,1)S(1)} %bitcast.10, bf16[192,16,256]{2,1,0:T(8,128)(2,1)S(1)} %bitcast.11, s32[192,128]{1,0:T(8,128)S(1)} %broadcast_in_dim.2.len_ref, ...), custom_call_target="tpu_custom_call" | custom-call | tf_op jit(solution)/shard_map/attend/pallas_call | solution.py:515
  41.0 0.0 copy-done.7
  41.0 0.0 copy-done.4
  41.0 0.0 copy-done.5
  41.1 0.0 copy-done.6
  41.1 0.0 copy-done.8
  41.1 0.0 copy-done.9
  41.1 114.9 %shard_map.158 = (bf16[4,192,384]{2,1,0:T(8,128)(2,1)S(1)}, bf16[4,192,384]{2,1,0:T(8,128)(2,1)S(1)}) custom-call(bf16[192,256]{1,0:T(8,128)(2,1)S(1)} %get-tuple-element.11.o_ref, bf16[1536,384]{1,0:T(8,128)(2,1)S(1)} %copy-done.4, bf16[256,384]{1,0:T(8,128)(2,1)S(1)} %copy-done.8, bf16[384,1536]{1,0:T(8,128)(2,1)S(1)} %copy-done.5, ...), custom_call_target="tpu_custom_call" | custom-call | flops 7000000000 | bytes 8000000 | tf_op jit(solution)/shard_map/pallas_call | solution.py:478
  156.0 1.1 shard_map.159
Async XLA Ops:
  1.5 34.2 %copy-start = (bf16[192,1,16,256]{3,2,1,0:T(8,128)(2,1)S(1)}, bf16[192,1,16,256]{3,2,1,0:T(8,128)(2,1)}, u32[]{:S(2)}) copy-start(bf16[192,1,16,256]{3,2,1,0:T(8,128)(2,1)} %param.15) | copy-start | bytes 4718596
  1.5 34.2 %copy-start.1 = (bf16[192,1,16,256]{3,2,1,0:T(8,128)(2,1)S(1)}, bf16[192,1,16,256]{3,2,1,0:T(8,128)(2,1)}, u32[]{:S(2)}) copy-start(bf16[192,1,16,256]{3,2,1,0:T(8,128)(2,1)} %param.16) | copy-start | bytes 4718596
  1.5 34.2 %copy-start.3 = (f32[2,16,128]{2,1,0:T(8,128)S(1)}, f32[2,16,128]{2,1,0:T(8,128)}, u32[]{:S(2)}) copy-start(f32[2,16,128]{2,1,0:T(8,128)} %constant.12.clone.tab_ref) | copy-start | bytes 49156
  1.5 39.5 %copy-start.7 = (bf16[1536,384]{1,0:T(8,128)(2,1)S(1)}, bf16[1536,384]{1,0:T(8,128)(2,1)}, u32[]{:S(2)}) copy-start(bf16[1536,384]{1,0:T(8,128)(2,1)} %wd_ref.1) | copy-start | bytes 3538948
  35.8 1.1 copy-start.2
  36.8 4.2 %copy-start.4 = (bf16[1536,384]{1,0:T(8,128)(2,1)S(1)}, bf16[1536,384]{1,0:T(8,128)(2,1)}, u32[]{:S(2)}) copy-start(bf16[1536,384]{1,0:T(8,128)(2,1)} %x_ref.3) | copy-start | bytes 3538948
  36.8 4.2 %copy-start.5 = (bf16[384,1536]{1,0:T(8,128)(2,1)S(1)}, bf16[384,1536]{1,0:T(8,128)(2,1)}, u32[]{:S(2)}) copy-start(bf16[384,1536]{1,0:T(8,128)(2,1)} %wg_ref.1) | copy-start | bytes 3538948
  36.8 4.2 %copy-start.6 = (bf16[384,1536]{1,0:T(8,128)(2,1)S(1)}, bf16[384,1536]{1,0:T(8,128)(2,1)}, u32[]{:S(2)}) copy-start(bf16[384,1536]{1,0:T(8,128)(2,1)} %wu_ref.1) | copy-start | bytes 3538948
  36.8 4.2 %copy-start.8 = (bf16[256,384]{1,0:T(8,128)(2,1)S(1)}, bf16[256,384]{1,0:T(8,128)(2,1)}, u32[]{:S(2)}) copy-start(bf16[256,384]{1,0:T(8,128)(2,1)} %wo_ref.1) | copy-start | bytes 589828
  36.9 4.2 %copy-start.9 = (f32[8,8,128]{2,1,0:T(8,128)S(1)}, f32[8,8,128]{2,1,0:T(8,128)}, u32[]{:S(2)}) copy-start(f32[8,8,128]{2,1,0:T(8,128)} %get-tuple-element.12.g_ref) | copy-start | bytes 98308

commit v4 on v3

--- a/solution.py
+++ b/solution.py
@@ -300,7 +300,7 @@
 
 
 def post_kernel(o_ref, x_ref, wo_ref, wg_ref, wu_ref, wd_ref, g_ref, u_out, v_out, o_buf, wo, x_o, wd, pa, pb, pc, pd, hs, ma, mb, acc_a, acc_b, w_gu, a_buf, u_buf, wait_buf, *rest):
-    rx, rx2, sems = rest[:14], rest[14:28], rest[28:]
+    rx, rx2, sems = rest[:14], rest[14:35], rest[35:]
     cm = Comm(wait_buf, sems)
     x, c, y, z = cm.x, cm.c, cm.y, cm.z
     (i, r, o, l), dr, dl = cm.rings['x']
@@ -378,27 +378,82 @@
         gelu = 0.5 * gate * (1.0 + jnp.tanh(0.7978845608 * (gate + 0.044715 * (gate * gate * gate))))
         a_buf[j, :, hcol(x)] = (gelu * up).astype(BF)
 
-    right, left = {}, {}
-    for j in (0, 2, 1, 3):
-        hidden(j)
-        own = a_buf.at[j, :, hcol(x)]
-        right[j] = cm.send(own, own, dr)
-        left[j] = cm.send(own, own, dl)
-    fwd = []
-    for j in (0, 1):
-        cm.wait(right[j])
-        src = a_buf.at[j, :, hcol(l)]
-        fwd.append(cm.send(src, src, dr))
-        cm.wait(left[j + 2])
-        src = a_buf.at[j + 2, :, hcol(r)]
-        fwd.append(cm.send(src, src, dl))
-    cm.wait(right[2], right[3], left[0], left[1], c_wd, own_wd)
-    for j, k in ((0, 0), (2, 1), (1, 2), (3, 3)):
-        cm.wait(fwd[k])
+    block = dict(zip('irol', cm.rings['z'][0]))
+    y_ring = cm.rings['y'][0]
+    ra, ra2, rb, rb2 = rx2[:12], rx2[12:15], rx2[15:18], rx2[18:21]
+    right, left, fwd, first, second = {}, {}, {}, {}, {}
+
+    def ship(name, via, dev):
+        own = a_buf.at[block[name], :, hcol(x)]
+        via[name] = cm.send(own, own, dev)
+
+    def pass_on(name, via, frm, dev):
+        cm.wait(via[name])
+        src = a_buf.at[block[name], :, hcol(frm)]
+        fwd[name] = cm.send(src, src, dev)
+
+    def down(name):
+        j = block[name]
         v = a_buf[j]
         pc[j] = jnp.dot(v, wd[0], preferred_element_type=F32)
         pd[j] = jnp.dot(v, wd[1], preferred_element_type=F32)
-    run(plane_scatter(cm, pc, 0, rx2[:7]), plane_scatter(cm, pd, 1, rx2[7:]))
+        k = 3 * 'orli'.index(name)
+        first[name] = direct4(cm, 'y', lambda q: pc.at[j, rows48(q)], lambda q: ra[k + q], cm.sems.pop())
+
+    def finish(name):
+        cm.wait(*first[name])
+        q = 3 * 'orli'.index(name)
+        pc[block[name], rows48(y)] += (ra[q][...] + ra[q + 2][...]) + ra[q + 1][...]
+
+    z_dev = {'o': cm.opposite['z'], 'r': cm.rings['z'][1], 'l': cm.rings['z'][2]}
+    slot = {'o': 1, 'r': 0, 'l': 2}
+
+    def send_z(name):
+        j = block[name]
+        second[name] = cm.send(pd.at[j], rb[slot[name]], z_dev[name])
+
+    def send_z2(name):
+        finish(name)
+        second[name + '2'] = cm.send(pc.at[block[name], rows48(y)], ra2[slot[name]], z_dev[name])
+
+    hidden(block['o'])
+    ship('o', right, dr)
+    hidden(block['r'])
+    ship('r', left, dl)
+    ship('o', left, dl)
+    hidden(block['l'])
+    ship('l', right, dr)
+    hidden(block['i'])
+    pass_on('o', right, l, dr)
+    ship('r', right, dr)
+    pass_on('r', left, r, dl)
+    ship('i', left, dl)
+    ship('l', left, dl)
+    pass_on('l', right, l, dr)
+    ship('i', right, dr)
+    cm.wait(c_wd, own_wd, left['o'], fwd['o'])
+    down('o')
+    send_z('o')
+    cm.wait(right['r'], fwd['r'])
+    pass_on('i', left, r, dl)
+    down('r')
+    send_z('r')
+    cm.wait(left['l'], fwd['l'])
+    down('l')
+    send_z('l')
+    send_z2('o')
+    send_z2('r')
+    cm.wait(right['i'], fwd['i'])
+    down('i')
+    cm.wait(second['o'], second['r'], second['l'])
+    pd[z] += (rb[0][...] + rb[2][...]) + rb[1][...]
+    last = direct_scatter(cm, 'y', lambda q: pd.at[z, rows48(q)], rb2)
+    next(last)
+    send_z2('l')
+    finish('i')
+    cm.wait(second['o2'], second['r2'], second['l2'])
+    pc[z, rows48(y)] += (ra2[0][...] + ra2[2][...]) + ra2[1][...]
+    run(last)
     u_buf[0, z, rows48(y, align=16)] = (hs[x, 0].astype(F32) + pc[z, rows48(y)]).astype(BF)
     u_buf[1, z, rows48(y, align=16)] = (hs[x, 1].astype(F32) + pd[z, rows48(y)]).astype(BF)
     run(plane_gather(cm, u_buf.at[0], 0), plane_gather(cm, u_buf.at[1], 1))
@@ -524,8 +579,8 @@
             [V((4, 192, 256), BF), V((2, 256, 384), BF), V((48, 384), BF), V((2, 1536, 384), BF)]
             + [V((4, 192, 384), F32)] * 4 + [V((4, 2, 48, 384), BF)] + [V((4, 192, 1536), BF)] * 2 + [V((4, 192, 768), F32)] * 2
             + [V((3072, 768), BF), V((4, 192, 1536), BF), V((2, 4, 192, 384), BF), V((16384, 128), BF)]
-            + scatter_scratch() + scatter_scratch(),
-            86, 1, 44, 7 * 10**9, 'vvvhhhv',
+            + scatter_scratch() + [V((48, 384), F32)] * 15 + [V((192, 384), F32)] * 3 + [V((48, 384), F32)] * 3,
+            89, 1, 44, 7 * 10**9, 'vvvhhhv',
             attn_out, resid_in, w_o, w_gate, w_up, w_down, gain_all)
         resid_out = pl.pallas_call(join_kernel, out_shape=sds((1536, 384), BF), in_specs=[VM, VM], out_specs=VM, compiler_params=pltpu.CompilerParams(vmem_limit_bytes=8 * 2**20))(mine, theirs)
         return resid_out, k_upd, v_upd

time: 157 us -> 152 us (0.968)
  Pallas kernels: 154 us -> 149 us
    pallas_call x1, Pallas kernels: 115 us -> 109 us  [call2(): pl.pallas_call(body, out_shape=outs[0] if single else outs, in_specs=[HB...]
where the time goes in v4:
time: 152 us
  Pallas kernels  149 us (98%)
  local copies, waits for them, and re-layouts  1.96 us (1%)
    pallas_call x1, Pallas kernels, call2(): pl.pallas_call(body, out_shape=outs[0] if single else outs, in_specs=[HB...  109 us
    pallas_call x1, Pallas kernels, call(): pl.pallas_call(body, out_shape=outs[0] if single else outs, in_specs=[HB...  34.2 us
    pallas_call x1, Pallas kernels, local_step(): pl.pallas_call(attend_kernel, name='attend', out_shape=(sds((192, 256), B...  4.18 us

profile of v4, /device:TPU:1, one launch (start us, length us, event | category | flops | bytes accessed | tf_op | source)
XLA Modules:
  0.0 151.6 jit_solution(5288908452848679541)
XLA Ops:
  0.6 0.8 dynamic_slice.3
  1.4 0.1 broadcast_in_dim.2.len_ref
  1.5 0.0 copy-start
  1.5 0.0 copy-start.1
  1.5 0.0 copy-start.3
  1.5 0.0 copy-start.7
  1.5 34.2 %shard_map.157 = (f32[3,192,256]{2,1,0:T(8,128)}, f32[8,8,128]{2,1,0:T(8,128)}) custom-call(bf16[1536,384]{1,0:T(8,128)(2,1)} %x_ref.3, bf16[384,256]{1,0:T(8,128)(2,1)} %wq_ref.1, bf16[384,256]{1,0:T(8,128)(2,1)} %wk_ref.1, bf16[384,256]{1,0:T(8,128)(2,1)} %wv_ref.1, bf16[3,128]{1,0:T(4,128)(2,1)} %bitcast.14, bf16[3,128]{1,0:T(4,128)(2,1)} %bitcast.15), custom_call_target="tpu_custom_call" | custom-call | flops 2000000000 | bytes 8000000 | tf_op jit(solution)/shard_map/pallas_call | solution.py:520
  35.7 0.0 copy-done
  35.8 0.0 copy-done.1
  35.8 0.0 copy-done.3
  35.8 0.0 copy-start.2
  35.8 1.1 copy-done.2
  36.8 0.0 copy-start.4
  36.8 0.0 copy-start.5
  36.8 0.0 copy-start.6
  36.8 0.0 copy-start.8
  36.9 0.0 copy-start.9
  36.9 4.2 %attend.1 = (bf16[192,256]{1,0:T(8,128)(2,1)S(1)}, bf16[192,16,256]{2,1,0:T(8,128)(2,1)}, bf16[192,16,256]{2,1,0:T(8,128)(2,1)}) custom-call(f32[3,192,256]{2,1,0:T(8,128)S(1)} %copy-done.2, bf16[192,16,256]{2,1,0:T(8,128)(2,1)S(1)} %bitcast.10, bf16[192,16,256]{2,1,0:T(8,128)(2,1)S(1)} %bitcast.11, s32[192,128]{1,0:T(8,128)S(1)} %broadcast_in_dim.2.len_ref, ...), custom_call_target="tpu_custom_call" | custom-call | tf_op jit(solution)/shard_map/attend/pallas_call | solution.py:570
  41.0 0.0 copy-done.7
  41.0 0.0 copy-done.4
  41.0 0.0 copy-done.5
  41.1 0.0 copy-done.6
  41.1 0.0 copy-done.8
  41.1 0.0 copy-done.9
  41.1 109.4 %shard_map.158 = (bf16[4,192,384]{2,1,0:T(8,128)(2,1)S(1)}, bf16[4,192,384]{2,1,0:T(8,128)(2,1)S(1)}) custom-call(bf16[192,256]{1,0:T(8,128)(2,1)S(1)} %get-tuple-element.11.o_ref, bf16[1536,384]{1,0:T(8,128)(2,1)S(1)} %copy-done.4, bf16[256,384]{1,0:T(8,128)(2,1)S(1)} %copy-done.8, bf16[384,1536]{1,0:T(8,128)(2,1)S(1)} %copy-done.5, ...), custom_call_target="tpu_custom_call" | custom-call | flops 7000000000 | bytes 8000000 | tf_op jit(solution)/shard_map/pallas_call | solution.py:533
  150.5 1.1 shard_map.159
Async XLA Ops:
  1.5 34.2 %copy-start = (bf16[192,1,16,256]{3,2,1,0:T(8,128)(2,1)S(1)}, bf16[192,1,16,256]{3,2,1,0:T(8,128)(2,1)}, u32[]{:S(2)}) copy-start(bf16[192,1,16,256]{3,2,1,0:T(8,128)(2,1)} %param.15) | copy-start | bytes 4718596
  1.5 34.2 %copy-start.1 = (bf16[192,1,16,256]{3,2,1,0:T(8,128)(2,1)S(1)}, bf16[192,1,16,256]{3,2,1,0:T(8,128)(2,1)}, u32[]{:S(2)}) copy-start(bf16[192,1,16,256]{3,2,1,0:T(8,128)(2,1)} %param.16) | copy-start | bytes 4718596
  1.5 34.2 %copy-start.3 = (f32[2,16,128]{2,1,0:T(8,128)S(1)}, f32[2,16,128]{2,1,0:T(8,128)}, u32[]{:S(2)}) copy-start(f32[2,16,128]{2,1,0:T(8,128)} %constant.12.clone.tab_ref) | copy-start | bytes 49156
  1.5 39.5 %copy-start.7 = (bf16[1536,384]{1,0:T(8,128)(2,1)S(1)}, bf16[1536,384]{1,0:T(8,128)(2,1)}, u32[]{:S(2)}) copy-start(bf16[1536,384]{1,0:T(8,128)(2,1)} %wd_ref.1) | copy-start | bytes 3538948
  35.8 1.1 copy-start.2
  36.8 4.2 %copy-start.4 = (bf16[1536,384]{1,0:T(8,128)(2,1)S(1)}, bf16[1536,384]{1,0:T(8,128)(2,1)}, u32[]{:S(2)}) copy-start(bf16[1536,384]{1,0:T(8,128)(2,1)} %x_ref.3) | copy-start | bytes 3538948
  36.8 4.2 %copy-start.5 = (bf16[384,1536]{1,0:T(8,128)(2,1)S(1)}, bf16[384,1536]{1,0:T(8,128)(2,1)}, u32[]{:S(2)}) copy-start(bf16[384,1536]{1,0:T(8,128)(2,1)} %wg_ref.1) | copy-start | bytes 3538948
  36.8 4.2 %copy-start.6 = (bf16[384,1536]{1,0:T(8,128)(2,1)S(1)}, bf16[384,1536]{1,0:T(8,128)(2,1)}, u32[]{:S(2)}) copy-start(bf16[384,1536]{1,0:T(8,128)(2,1)} %wu_ref.1) | copy-start | bytes 3538948
  36.8 4.2 %copy-start.8 = (bf16[256,384]{1,0:T(8,128)(2,1)S(1)}, bf16[256,384]{1,0:T(8,128)(2,1)}, u32[]{:S(2)}) copy-start(bf16[256,384]{1,0:T(8,128)(2,1)} %wo_ref.1) | copy-start | bytes 589828
  36.9 4.2 %copy-start.9 = (f32[8,8,128]{2,1,0:T(8,128)S(1)}, f32[8,8,128]{2,1,0:T(8,128)}, u32[]{:S(2)}) copy-start(f32[8,8,128]{2,1,0:T(8,128)} %get-tuple-element.12.g_ref) | copy-start | bytes 98308

commit v5 on v4

--- a/solution.py
+++ b/solution.py
@@ -159,14 +159,29 @@
     return [V((2, 48, 384), F32)] * 2 + [V((4, 48, 384), F32)] * 2 + small + [V((96, 384), F32)] * 2 + [V((192, 384), F32)] * 2 + small
 
 
-def plane_gather(cm, m, h):
+def plane_burst(cm, m, h):
     at = lambda j: rows48(j, align=16)
-    if h == 0:
-        yield from direct_gather(cm, 'y', lambda j: m.at[cm.z, at(j)])
-        yield from direct_gather(cm, 'z', lambda j: m.at[j])
-    else:
-        yield from direct_gather(cm, 'z', lambda j: m.at[j, at(cm.y)])
-        yield from direct_gather(cm, 'y', lambda j: m.at[:, at(j)])
+    first, second = ('y', 'z') if h == 0 else ('z', 'y')
+    piece = (lambda k: m.at[cm.z, at(k)]) if h == 0 else (lambda k: m.at[k, at(cm.y)])
+    ki, kr, ko, kl = cm.rings[first][0]
+    recv = cm.sems.pop()
+    outs = []
+
+    def out(k):
+        outs.extend(direct4(cm, second, lambda j: piece(k), lambda q: piece(k), recv))
+
+    small = direct4(cm, first, lambda j: piece(ki), lambda k: piece(ki))
+    out(ki)
+    yield
+    cm.wait(small[1])
+    out(kl)
+    cm.wait(small[2])
+    out(kr)
+    yield
+    cm.wait(small[0])
+    out(ko)
+    yield
+    cm.wait(*outs)
 
 
 def plane_stream(cm, m, h, near):
@@ -293,8 +308,11 @@
     add(l)
     cm.wait(e2)
     add(r)
-    cm.wait(*f0, *f1)
-    cm.wait(cm.send(rows(o), rows(o), dev_o))
+    late = []
+    for cp, (n, p) in zip(f0 + f1, pieces[:2] + pieces[:1:-1]):
+        cm.wait(cp)
+        late.append(cm.send(rows(o).at[n, p], rows(o).at[n, p], dev_o))
+    cm.wait(*late)
     add(o)
     cm.drain()
 
@@ -332,19 +350,19 @@
         yield
         cm.wait(*here)
 
+    def o_proj(j):
+        v = o_buf[j]
+        pa[j] = jnp.dot(v, wo[0], preferred_element_type=F32)
+        pb[j] = jnp.dot(v, wo[1], preferred_element_type=F32)
+
+    cm.wait(c_wo)
+    o_proj(i)
     for _ in go:
         pass
     deal_g = deal(wg_ref, 0, 3)
     next(deal_g)
-    cm.wait(c_wo)
-
-    def o_proj(j, carry):
-        v = o_buf[j]
-        pa[j] = jnp.dot(v, wo[0], preferred_element_type=F32)
-        pb[j] = jnp.dot(v, wo[1], preferred_element_type=F32)
-        return carry
-
-    lax.fori_loop(0, 4, o_proj, 0)
+    for j in (r, o, l):
+        o_proj(j)
     run(plane_scatter(cm, pa, 0, rx[:7]), plane_scatter(cm, pb, 1, rx[7:]), deal_g)
 
     cm.wait(c_x)
@@ -453,10 +471,15 @@
     finish('i')
     cm.wait(second['o2'], second['r2'], second['l2'])
     pc[z, rows48(y)] += (ra2[0][...] + ra2[2][...]) + ra2[1][...]
+    at = rows48(y, align=16)
+    u_buf[0, z, at] = (hs[x, 0].astype(F32) + pc[z, rows48(y)]).astype(BF)
+    half0 = plane_burst(cm, u_buf.at[0], 0)
+    next(half0)
     run(last)
-    u_buf[0, z, rows48(y, align=16)] = (hs[x, 0].astype(F32) + pc[z, rows48(y)]).astype(BF)
-    u_buf[1, z, rows48(y, align=16)] = (hs[x, 1].astype(F32) + pd[z, rows48(y)]).astype(BF)
-    run(plane_gather(cm, u_buf.at[0], 0), plane_gather(cm, u_buf.at[1], 1))
+    u_buf[1, z, at] = (hs[x, 1].astype(F32) + pd[z, rows48(y)]).astype(BF)
+    half1 = plane_burst(cm, u_buf.at[1], 1)
+    next(half1)
+    run(half0, half1)
     c_v = cm.send(u_buf.at[1 - c], v_out, dev_o)
     u_out[...] = u_buf[c]
     cm.wait(c_v)
@@ -506,7 +529,7 @@
         lanes = slice(128 * n, 128 * n + 128)
         v = jnp.where(hit, v_new[n], vc_ref[at, :, lanes].astype(F32))
         vu_ref[:, :, lanes] = v.astype(BF)
-        o_ref[:, lanes] = jnp.sum(jnp.where(slot <= pos3, p * v, 0.0), axis=1).astype(BF)
+        o_ref[:, lanes] = jnp.sum(p * v, axis=1).astype(BF)
 
 
 VM = pl.BlockSpec(memory_space=pltpu.VMEM)
@@ -563,7 +586,7 @@
             qkv_kernel,
             (sds((3, 192, 256), F32), sds((8, 8, 128), F32)),
             [V((8, 3, 384, 256), BF), V((2, 4, 4, 4, 16, 384), BF), V((8, 192, 384), BF), V((8, 128), F32), V((8192, 128), BF)],
-            37, 0, 58, 2 * 10**9, 'hhhhvv',
+            40, 0, 58, 2 * 10**9, 'hhhhvv',
             resid_in, w_q, w_k, w_v, norm_attn.reshape(3, 128), norm_mlp.reshape(3, 128))
         lengths = lax.dynamic_slice_in_dim(cache_len, lax.axis_index('dm') * 192, 192)
         cache, step = sds((192, 16, 256), BF), 48
@@ -580,7 +603,7 @@
             + [V((4, 192, 384), F32)] * 4 + [V((4, 2, 48, 384), BF)] + [V((4, 192, 1536), BF)] * 2 + [V((4, 192, 768), F32)] * 2
             + [V((3072, 768), BF), V((4, 192, 1536), BF), V((2, 4, 192, 384), BF), V((16384, 128), BF)]
             + scatter_scratch() + [V((48, 384), F32)] * 15 + [V((192, 384), F32)] * 3 + [V((48, 384), F32)] * 3,
-            89, 1, 44, 7 * 10**9, 'vvvhhhv',
+            93, 1, 44, 7 * 10**9, 'vvvhhhv',
             attn_out, resid_in, w_o, w_gate, w_up, w_down, gain_all)
         resid_out = pl.pallas_call(join_kernel, out_shape=sds((1536, 384), BF), in_specs=[VM, VM], out_specs=VM, compiler_params=pltpu.CompilerParams(vmem_limit_bytes=8 * 2**20))(mine, theirs)
         return resid_out, k_upd, v_upd

time: 152 us -> 150 us (0.987)
  Pallas kernels: 149 us -> 147 us
where the time goes in v5:
time: 150 us
  Pallas kernels  147 us (98%)
  local copies, waits for them, and re-layouts  1.96 us (1%)
    pallas_call x1, Pallas kernels, call2(): pl.pallas_call(body, out_shape=outs[0] if single else outs, in_specs=[HB...  108 us
    pallas_call x1, Pallas kernels, call(): pl.pallas_call(body, out_shape=outs[0] if single else outs, in_specs=[HB...  34.2 us
    pallas_call x1, Pallas kernels, local_step(): pl.pallas_call(attend_kernel, name='attend', out_shape=(sds((192, 256), B...  4.17 us

profile of v5, /device:TPU:1, one launch (start us, length us, event | category | flops | bytes accessed | tf_op | source)
XLA Modules:
  0.0 150.1 jit_solution(15194142751987397458)
XLA Ops:
  0.6 0.8 dynamic_slice.3
  1.4 0.1 broadcast_in_dim.2.len_ref
  1.5 0.0 copy-start
  1.5 0.0 copy-start.1
  1.5 0.0 copy-start.3
  1.5 0.0 copy-start.7
  1.5 34.2 %shard_map.157 = (f32[3,192,256]{2,1,0:T(8,128)}, f32[8,8,128]{2,1,0:T(8,128)}) custom-call(bf16[1536,384]{1,0:T(8,128)(2,1)} %x_ref.3, bf16[384,256]{1,0:T(8,128)(2,1)} %wq_ref.1, bf16[384,256]{1,0:T(8,128)(2,1)} %wk_ref.1, bf16[384,256]{1,0:T(8,128)(2,1)} %wv_ref.1, bf16[3,128]{1,0:T(4,128)(2,1)} %bitcast.14, bf16[3,128]{1,0:T(4,128)(2,1)} %bitcast.15), custom_call_target="tpu_custom_call" | custom-call | flops 2000000000 | bytes 8000000 | tf_op jit(solution)/shard_map/pallas_call | solution.py:543
  35.8 0.0 copy-done
  35.8 0.0 copy-done.1
  35.8 0.0 copy-done.3
  35.8 0.0 copy-start.2
  35.8 1.1 copy-done.2
  36.9 0.0 copy-start.4
  36.9 0.0 copy-start.5
  36.9 0.0 copy-start.6
  36.9 0.0 copy-start.8
  36.9 0.0 copy-start.9
  36.9 4.2 %attend.1 = (bf16[192,256]{1,0:T(8,128)(2,1)S(1)}, bf16[192,16,256]{2,1,0:T(8,128)(2,1)}, bf16[192,16,256]{2,1,0:T(8,128)(2,1)}) custom-call(f32[3,192,256]{2,1,0:T(8,128)S(1)} %copy-done.2, bf16[192,16,256]{2,1,0:T(8,128)(2,1)S(1)} %bitcast.10, bf16[192,16,256]{2,1,0:T(8,128)(2,1)S(1)} %bitcast.11, s32[192,128]{1,0:T(8,128)S(1)} %broadcast_in_dim.2.len_ref, ...), custom_call_target="tpu_custom_call" | custom-call | tf_op jit(solution)/shard_map/attend/pallas_call | solution.py:593
  41.1 0.0 copy-done.7
  41.1 0.0 copy-done.4
  41.1 0.0 copy-done.5
  41.1 0.0 copy-done.6
  41.1 0.0 copy-done.8
  41.1 0.0 copy-done.9
  41.1 107.9 %shard_map.158 = (bf16[4,192,384]{2,1,0:T(8,128)(2,1)S(1)}, bf16[4,192,384]{2,1,0:T(8,128)(2,1)S(1)}) custom-call(bf16[192,256]{1,0:T(8,128)(2,1)S(1)} %get-tuple-element.11.o_ref, bf16[1536,384]{1,0:T(8,128)(2,1)S(1)} %copy-done.4, bf16[256,384]{1,0:T(8,128)(2,1)S(1)} %copy-done.8, bf16[384,1536]{1,0:T(8,128)(2,1)S(1)} %copy-done.5, ...), custom_call_target="tpu_custom_call" | custom-call | flops 7000000000 | bytes 8000000 | tf_op jit(solution)/shard_map/pallas_call | solution.py:556
  149.0 1.1 shard_map.159
Async XLA Ops:
  1.5 34.3 %copy-start = (bf16[192,1,16,256]{3,2,1,0:T(8,128)(2,1)S(1)}, bf16[192,1,16,256]{3,2,1,0:T(8,128)(2,1)}, u32[]{:S(2)}) copy-start(bf16[192,1,16,256]{3,2,1,0:T(8,128)(2,1)} %param.15) | copy-start | bytes 4718596
  1.5 34.3 %copy-start.1 = (bf16[192,1,16,256]{3,2,1,0:T(8,128)(2,1)S(1)}, bf16[192,1,16,256]{3,2,1,0:T(8,128)(2,1)}, u32[]{:S(2)}) copy-start(bf16[192,1,16,256]{3,2,1,0:T(8,128)(2,1)} %param.16) | copy-start | bytes 4718596
  1.5 34.3 %copy-start.3 = (f32[2,16,128]{2,1,0:T(8,128)S(1)}, f32[2,16,128]{2,1,0:T(8,128)}, u32[]{:S(2)}) copy-start(f32[2,16,128]{2,1,0:T(8,128)} %constant.12.clone.tab_ref) | copy-start | bytes 49156
  1.5 39.5 %copy-start.7 = (bf16[1536,384]{1,0:T(8,128)(2,1)S(1)}, bf16[1536,384]{1,0:T(8,128)(2,1)}, u32[]{:S(2)}) copy-start(bf16[1536,384]{1,0:T(8,128)(2,1)} %wd_ref.1) | copy-start | bytes 3538948
  35.8 1.1 copy-start.2
  36.9 4.2 %copy-start.4 = (bf16[1536,384]{1,0:T(8,128)(2,1)S(1)}, bf16[1536,384]{1,0:T(8,128)(2,1)}, u32[]{:S(2)}) copy-start(bf16[1536,384]{1,0:T(8,128)(2,1)} %x_ref.3) | copy-start | bytes 3538948
  36.9 4.2 %copy-start.5 = (bf16[384,1536]{1,0:T(8,128)(2,1)S(1)}, bf16[384,1536]{1,0:T(8,128)(2,1)}, u32[]{:S(2)}) copy-start(bf16[384,1536]{1,0:T(8,128)(2,1)} %wg_ref.1) | copy-start | bytes 3538948
  36.9 4.2 %copy-start.6 = (bf16[384,1536]{1,0:T(8,128)(2,1)S(1)}, bf16[384,1536]{1,0:T(8,128)(2,1)}, u32[]{:S(2)}) copy-start(bf16[384,1536]{1,0:T(8,128)(2,1)} %wu_ref.1) | copy-start | bytes 3538948
  36.9 4.2 %copy-start.8 = (bf16[256,384]{1,0:T(8,128)(2,1)S(1)}, bf16[256,384]{1,0:T(8,128)(2,1)}, u32[]{:S(2)}) copy-start(bf16[256,384]{1,0:T(8,128)(2,1)} %wo_ref.1) | copy-start | bytes 589828
  36.9 4.2 %copy-start.9 = (f32[8,8,128]{2,1,0:T(8,128)S(1)}, f32[8,8,128]{2,1,0:T(8,128)}, u32[]{:S(2)}) copy-start(f32[8,8,128]{2,1,0:T(8,128)} %get-tuple-element.12.g_ref) | copy-start | bytes 98308

commit v6 on v5

--- a/solution.py
+++ b/solution.py
@@ -458,16 +458,29 @@
     send_z('r')
     cm.wait(left['l'], fwd['l'])
     down('l')
-    send_z('l')
+    y_row = dict(zip('irol', y_ring))
+    third = {q: cm.send(pd.at[block['l'], rows48(y_row[q])], rb[2].at[rows48(y_row[q])], z_dev['l']) for q in 'orli'}
     send_z2('o')
     send_z2('r')
     cm.wait(right['i'], fwd['i'])
     down('i')
-    cm.wait(second['o'], second['r'], second['l'])
-    pd[z] += (rb[0][...] + rb[2][...]) + rb[1][...]
-    last = direct_scatter(cm, 'y', lambda q: pd.at[z, rows48(q)], rb2)
-    next(last)
+    cm.wait(second['o'], second['r'])
+    pd[z] += rb[0][...] + rb[1][...]
+    y_dev = {'o': cm.opposite['y'], 'r': cm.rings['y'][1], 'l': cm.rings['y'][2]}
+    recv = cm.sems.pop()
+    last = []
+
+    def third_piece(q):
+        cm.wait(third[q])
+        pd[z, rows48(y_row[q])] += rb[2][rows48(y_row[q]), :]
+        if q != 'i':
+            last.append(cm.send(pd.at[z, rows48(y_row[q])], rb2[slot[q]], y_dev[q], recv))
+
+    third_piece('o')
+    third_piece('r')
     send_z2('l')
+    third_piece('l')
+    third_piece('i')
     finish('i')
     cm.wait(second['o2'], second['r2'], second['l2'])
     pc[z, rows48(y)] += (ra2[0][...] + ra2[2][...]) + ra2[1][...]
@@ -475,7 +488,8 @@
     u_buf[0, z, at] = (hs[x, 0].astype(F32) + pc[z, rows48(y)]).astype(BF)
     half0 = plane_burst(cm, u_buf.at[0], 0)
     next(half0)
-    run(last)
+    cm.wait(*last)
+    pd[z, rows48(y)] += (rb2[0][...] + rb2[2][...]) + rb2[1][...]
     u_buf[1, z, at] = (hs[x, 1].astype(F32) + pd[z, rows48(y)]).astype(BF)
     half1 = plane_burst(cm, u_buf.at[1], 1)
     next(half1)
@@ -603,7 +617,7 @@
             + [V((4, 192, 384), F32)] * 4 + [V((4, 2, 48, 384), BF)] + [V((4, 192, 1536), BF)] * 2 + [V((4, 192, 768), F32)] * 2
             + [V((3072, 768), BF), V((4, 192, 1536), BF), V((2, 4, 192, 384), BF), V((16384, 128), BF)]
             + scatter_scratch() + [V((48, 384), F32)] * 15 + [V((192, 384), F32)] * 3 + [V((48, 384), F32)] * 3,
-            93, 1, 44, 7 * 10**9, 'vvvhhhv',
+            96, 1, 44, 7 * 10**9, 'vvvhhhv',
             attn_out, resid_in, w_o, w_gate, w_up, w_down, gain_all)
         resid_out = pl.pallas_call(join_kernel, out_shape=sds((1536, 384), BF), in_specs=[VM, VM], out_specs=VM, compiler_params=pltpu.CompilerParams(vmem_limit_bytes=8 * 2**20))(mine, theirs)
         return resid_out, k_upd, v_upd

time: 150 us -> 150 us (level)
  no operation moved by 1% of the time
where the time goes in v6:
time: 150 us
  Pallas kernels  147 us (98%)
  local copies, waits for them, and re-layouts  1.96 us (1%)
    pallas_call x1, Pallas kernels, call2(): pl.pallas_call(body, out_shape=outs[0] if single else outs, in_specs=[HB...  108 us
    pallas_call x1, Pallas kernels, call(): pl.pallas_call(body, out_shape=outs[0] if single else outs, in_specs=[HB...  34.2 us
    pallas_call x1, Pallas kernels, local_step(): pl.pallas_call(attend_kernel, name='attend', out_shape=(sds((192, 256), B...  4.17 us

profile of v6, /device:TPU:1, one launch (start us, length us, event | category | flops | bytes accessed | tf_op | source)
XLA Modules:
  0.0 150.2 jit_solution(15366689046249161405)
XLA Ops:
  0.6 0.8 dynamic_slice.3
  1.4 0.1 broadcast_in_dim.2.len_ref
  1.5 0.0 copy-start
  1.5 0.0 copy-start.1
  1.5 0.0 copy-start.3
  1.5 0.0 copy-start.7
  1.5 34.2 %shard_map.157 = (f32[3,192,256]{2,1,0:T(8,128)}, f32[8,8,128]{2,1,0:T(8,128)}) custom-call(bf16[1536,384]{1,0:T(8,128)(2,1)} %x_ref.3, bf16[384,256]{1,0:T(8,128)(2,1)} %wq_ref.1, bf16[384,256]{1,0:T(8,128)(2,1)} %wk_ref.1, bf16[384,256]{1,0:T(8,128)(2,1)} %wv_ref.1, bf16[3,128]{1,0:T(4,128)(2,1)} %bitcast.14, bf16[3,128]{1,0:T(4,128)(2,1)} %bitcast.15), custom_call_target="tpu_custom_call" | custom-call | flops 2000000000 | bytes 8000000 | tf_op jit(solution)/shard_map/pallas_call | solution.py:557
  35.8 0.0 copy-done
  35.8 0.0 copy-done.1
  35.8 0.0 copy-done.3
  35.8 0.0 copy-start.2
  35.8 1.1 copy-done.2
  36.9 0.0 copy-start.4
  36.9 0.0 copy-start.5
  36.9 0.0 copy-start.6
  36.9 0.0 copy-start.8
  36.9 0.0 copy-start.9
  36.9 4.2 %attend.1 = (bf16[192,256]{1,0:T(8,128)(2,1)S(1)}, bf16[192,16,256]{2,1,0:T(8,128)(2,1)}, bf16[192,16,256]{2,1,0:T(8,128)(2,1)}) custom-call(f32[3,192,256]{2,1,0:T(8,128)S(1)} %copy-done.2, bf16[192,16,256]{2,1,0:T(8,128)(2,1)S(1)} %bitcast.10, bf16[192,16,256]{2,1,0:T(8,128)(2,1)S(1)} %bitcast.11, s32[192,128]{1,0:T(8,128)S(1)} %broadcast_in_dim.2.len_ref, ...), custom_call_target="tpu_custom_call" | custom-call | tf_op jit(solution)/shard_map/attend/pallas_call | solution.py:607
  41.1 0.0 copy-done.7
  41.1 0.0 copy-done.4
  41.1 0.0 copy-done.5
  41.1 0.0 copy-done.6
  41.1 0.0 copy-done.8
  41.1 0.0 copy-done.9
  41.1 107.9 %shard_map.158 = (bf16[4,192,384]{2,1,0:T(8,128)(2,1)S(1)}, bf16[4,192,384]{2,1,0:T(8,128)(2,1)S(1)}) custom-call(bf16[192,256]{1,0:T(8,128)(2,1)S(1)} %get-tuple-element.11.o_ref, bf16[1536,384]{1,0:T(8,128)(2,1)S(1)} %copy-done.4, bf16[256,384]{1,0:T(8,128)(2,1)S(1)} %copy-done.8, bf16[384,1536]{1,0:T(8,128)(2,1)S(1)} %copy-done.5, ...), custom_call_target="tpu_custom_call" | custom-call | flops 7000000000 | bytes 8000000 | tf_op jit(solution)/shard_map/pallas_call | solution.py:570
  149.0 1.1 shard_map.159
Async XLA Ops:
  1.5 34.3 %copy-start = (bf16[192,1,16,256]{3,2,1,0:T(8,128)(2,1)S(1)}, bf16[192,1,16,256]{3,2,1,0:T(8,128)(2,1)}, u32[]{:S(2)}) copy-start(bf16[192,1,16,256]{3,2,1,0:T(8,128)(2,1)} %param.15) | copy-start | bytes 4718596
  1.5 34.3 %copy-start.1 = (bf16[192,1,16,256]{3,2,1,0:T(8,128)(2,1)S(1)}, bf16[192,1,16,256]{3,2,1,0:T(8,128)(2,1)}, u32[]{:S(2)}) copy-start(bf16[192,1,16,256]{3,2,1,0:T(8,128)(2,1)} %param.16) | copy-start | bytes 4718596
  1.5 34.3 %copy-start.3 = (f32[2,16,128]{2,1,0:T(8,128)S(1)}, f32[2,16,128]{2,1,0:T(8,128)}, u32[]{:S(2)}) copy-start(f32[2,16,128]{2,1,0:T(8,128)} %constant.12.clone.tab_ref) | copy-start | bytes 49156
  1.5 39.5 %copy-start.7 = (bf16[1536,384]{1,0:T(8,128)(2,1)S(1)}, bf16[1536,384]{1,0:T(8,128)(2,1)}, u32[]{:S(2)}) copy-start(bf16[1536,384]{1,0:T(8,128)(2,1)} %wd_ref.1) | copy-start | bytes 3538948
  35.8 1.1 copy-start.2
  36.9 4.2 %copy-start.4 = (bf16[1536,384]{1,0:T(8,128)(2,1)S(1)}, bf16[1536,384]{1,0:T(8,128)(2,1)}, u32[]{:S(2)}) copy-start(bf16[1536,384]{1,0:T(8,128)(2,1)} %x_ref.3) | copy-start | bytes 3538948
  36.9 4.2 %copy-start.5 = (bf16[384,1536]{1,0:T(8,128)(2,1)S(1)}, bf16[384,1536]{1,0:T(8,128)(2,1)}, u32[]{:S(2)}) copy-start(bf16[384,1536]{1,0:T(8,128)(2,1)} %wg_ref.1) | copy-start | bytes 3538948
  36.9 4.2 %copy-start.6 = (bf16[384,1536]{1,0:T(8,128)(2,1)S(1)}, bf16[384,1536]{1,0:T(8,128)(2,1)}, u32[]{:S(2)}) copy-start(bf16[384,1536]{1,0:T(8,128)(2,1)} %wu_ref.1) | copy-start | bytes 3538948
  36.9 4.2 %copy-start.8 = (bf16[256,384]{1,0:T(8,128)(2,1)S(1)}, bf16[256,384]{1,0:T(8,128)(2,1)}, u32[]{:S(2)}) copy-start(bf16[256,384]{1,0:T(8,128)(2,1)} %wo_ref.1) | copy-start | bytes 589828
  36.9 4.2 %copy-start.9 = (f32[8,8,128]{2,1,0:T(8,128)S(1)}, f32[8,8,128]{2,1,0:T(8,128)}, u32[]{:S(2)}) copy-start(f32[8,8,128]{2,1,0:T(8,128)} %get-tuple-element.12.g_ref) | copy-start | bytes 98308
